TPU v7x, 32 devices: a whole 2x2x4 slice. The times are simulated.
32 devices in a mesh: tok: 8 (over z, y), head: 4 (over x, core).
Axes of the slice: x: 2, y: 2, z: 4, core: 2. Of those that a mesh axis runs over, the one named last changes fastest.
Arguments:
- query_rows: bfloat16 [4096, 4, 1024], P('tok', 'head'), may hold values from -6 to 6
- key_rows: bfloat16 [4096, 4, 128], P('tok', 'head'), may hold values from -6 to 6
- value_rows: bfloat16 [4096, 4, 128], P('tok', 'head'), may hold values from -6 to 6
- output_gradient: bfloat16 [4096, 4, 1024], P('tok', 'head'), may hold values from -6 to 6
- row_logsumexp: bfloat16 [4, 8, 4096], P('head', None, 'tok'), may hold values from 3 to 7
- row_delta_sums: bfloat16 [4, 8, 4096], P('head', None, 'tok'), may hold values from -5 to 5
- segments: int32 [4096], replicated, may hold values from 0 to 4095, as said below
- query_key_value_weight: bfloat16 [4096, 4, 1280], P('tok', 'head'), may hold values from -0.09375 to 0.09375
Outputs:
- grad_input: bfloat16 [4096, 4096], P('tok', 'head')
Inputs may be any that keep to these rules, and one draw needn't show every extreme that they name: `segments`: numbers never fall along the tokens, and every document lies inside one window of 512 consecutive tokens.
All inputs are finite; a program needn't handle non-finite values.
Results may differ from a plain program's by a relative error of at most 0.012.
Values may be sent and summed in bfloat16 or wider, within the bound.
A program may use at most 128 MiB of HBM per device.

v0:
```python
import functools

import jax
import jax.numpy as jnp
import numpy as np
from jax import lax
from jax.experimental import pallas as pl
from jax.experimental.pallas import tpu as pltpu
from jax.sharding import PartitionSpec as P

BLOCK = 128


def pair_lists(block_count):
    query_list = []
    key_list = []
    for query_block in range(block_count):
        for key_block in range(query_block + 1):
            query_list.append(query_block)
            key_list.append(key_block)
    return (np.array(query_list, np.int32), np.array(key_list, np.int32))


def live_pairs(seg_window, query_list, key_list, tile_rows):
    first_seg = jnp.take(seg_window, query_list * tile_rows)
    last_seg = jnp.take(seg_window, key_list * tile_rows + tile_rows - 1)
    return (first_seg == last_seg) | jnp.asarray(query_list == key_list)


def pair_grads(query_tile, dout_tile, key_tile, value_tile, lse_tile, delta_tile, allowed):
    tile_rows, groups, query_width = query_tile.shape
    head_size = key_tile.shape[2]
    heads_per_group = query_width // head_size
    query_heads = query_tile.reshape(tile_rows, groups, heads_per_group, head_size)
    dout_heads = dout_tile.reshape(tile_rows, groups, heads_per_group, head_size)
    scores = jnp.einsum(
        "agrd,bgd->grab", query_heads, key_tile, preferred_element_type=jnp.float32
    ) * head_size ** (-0.5)
    logits = scores - lse_tile.astype(jnp.float32)[:, :, :, None]
    soft_probs = jnp.where(allowed[None, None], jnp.exp(logits), 0.0)
    probs_low = soft_probs.astype(jnp.bfloat16)
    value_gradient = jnp.einsum(
        "grab,agrd->bgd", probs_low, dout_heads, preferred_element_type=jnp.float32
    )
    grad_prob = jnp.einsum(
        "agrd,bgd->grab", dout_heads, value_tile, preferred_element_type=jnp.float32
    )
    grad_score = (soft_probs * (grad_prob - delta_tile.astype(jnp.float32)[:, :, :, None])).astype(
        jnp.bfloat16
    )
    query_gradient = jnp.einsum(
        "grab,bgd->agrd", grad_score, key_tile, preferred_element_type=jnp.float32
    )
    key_gradient = jnp.einsum(
        "grab,agrd->bgd", grad_score, query_heads, preferred_element_type=jnp.float32
    )
    return (query_gradient.reshape(tile_rows, groups, query_width), key_gradient, value_gradient)


def on_device(
    query_rows,
    key_rows,
    value_rows,
    output_gradient,
    row_logsumexp,
    row_delta_sums,
    segments,
    query_key_value_weight,
):
    window, kv_dev, query_width = query_rows.shape
    head_size = key_rows.shape[2]
    tile_rows = BLOCK
    block_count = window // tile_rows
    query_list, key_list = pair_lists(block_count)
    query_table = jnp.asarray(query_list)
    key_table = jnp.asarray(key_list)
    myself = lax.axis_index("tok")
    own_seg = lax.dynamic_slice_in_dim(segments, myself * window, window)
    own_live = live_pairs(own_seg, query_list, key_list, tile_rows)
    block_ids = jnp.arange(block_count, dtype=jnp.int32)
    query_match = (query_table[:, None] == block_ids[None, :]) & own_live[:, None]
    key_match = key_table[:, None] == block_ids[None, :]
    block_local = jnp.any(query_match[:, :, None] & key_match[:, None, :], axis=0)
    token_local = jnp.repeat(jnp.repeat(block_local, tile_rows, axis=0), tile_rows, axis=1)
    offsets = jnp.arange(window, dtype=jnp.int32)
    allowed_all = (
        (own_seg[:, None] == own_seg[None, :])
        & (offsets[None, :] <= offsets[:, None])
        & token_local
    )
    local_out = pair_grads(
        query_rows,
        output_gradient,
        key_rows,
        value_rows,
        row_logsumexp,
        row_delta_sums,
        allowed_all,
    )
    acc_query = local_out[0].reshape(block_count, tile_rows, kv_dev, query_width)
    acc_key = local_out[1].reshape(block_count, tile_rows, kv_dev, head_size)
    acc_value = local_out[2].reshape(block_count, tile_rows, kv_dev, head_size)
    score_scale = head_size ** (-0.5)
    query_gradient = (acc_query * score_scale).reshape(window, kv_dev, query_width)
    key_gradient = (acc_key * score_scale).reshape(window, kv_dev, head_size)
    value_gradient = acc_value.reshape(window, kv_dev, head_size)
    stacked_gradients = (
        jnp.concatenate([query_gradient, key_gradient, value_gradient], axis=2)
        .astype(jnp.bfloat16)
        .reshape(window, -1)
    )
    weight_piece = lax.all_gather(query_key_value_weight, "tok", axis=0, tiled=True)
    flat_piece = weight_piece.reshape(weight_piece.shape[0], -1)
    partial_sum = lax.dot_general(
        stacked_gradients, flat_piece, (((1,), (1,)), ((), ())), preferred_element_type=jnp.float32
    )
    summed = lax.psum_scatter(
        partial_sum.astype(jnp.bfloat16), "head", scatter_dimension=1, tiled=True
    )
    return summed


MESH = pl.DeviceIdType.MESH
LANES = 128


def fused_kernel(
    inner,
    q_ref,
    k_ref,
    v_ref,
    do_ref,
    lse_ref,
    delta_ref,
    seg_ref,
    w_ref,
    out_ref,
    joined,
    w_all,
    part,
    got,
    fwd_out,
    fwd_in,
    bias,
    lse32,
    delta32,
    dk_acc,
    dv_acc,
    w_send,
    w_recv,
    j_send,
    j_recv,
    p_send,
    p_recv,
    f_send,
    f_recv,
):
    outer, chunks = w_all.shape[0], w_all.shape[1]
    heads = outer
    window, head_size = k_ref.shape
    groups = q_ref.shape[1] // head_size
    rows = w_ref.shape[0]
    tok, h = lax.axis_index("tok"), lax.axis_index("head")
    z, y = tok // inner, tok % inner
    yo = inner - 1 - y

    def remote(src, dst, send, recv, to_tok, to_head):
        return pltpu.make_async_remote_copy(
            src_ref=src,
            dst_ref=dst,
            send_sem=send,
            recv_sem=recv,
            device_id=(to_tok, to_head),
            device_id_type=MESH,
        )

    def peer(step):
        return lax.rem(h + step, heads)

    barrier = pltpu.get_barrier_semaphore()
    pl.semaphore_signal(barrier, inc=1, device_id=(z * inner + yo, h), device_id_type=MESH)
    for step in range(1, heads):
        for to_y in (y, yo):
            pl.semaphore_signal(
                barrier, inc=1, device_id=(z * inner + to_y, peer(step)), device_id_type=MESH
            )

    @pl.when(z > 0)
    def _():
        pl.semaphore_signal(barrier, inc=1, device_id=(tok - inner, h), device_id_type=MESH)

    @pl.when(z < outer - 1)
    def _():
        pl.semaphore_signal(barrier, inc=1, device_id=(tok + inner, h), device_id_type=MESH)

    edges = jnp.where(z > 0, 1, 0) + jnp.where(z < outer - 1, 1, 0)
    pl.semaphore_wait(barrier, 2 * heads - 1 + edges)

    def own_w(c):
        return pl.ds(pl.multiple_of(c * LANES, LANES), LANES)

    def w_copy(side, o, c, own):
        src = w_ref.at[own_w(c)] if own else w_all.at[o, c]
        move = 1 if side == 1 else -1
        return remote(
            src, w_all.at[o, c], w_send.at[side, o, c], w_recv.at[o, c], tok + move * inner, h
        )

    def can_send(side):
        return z < outer - 1 if side == 1 else z > 0

    def each_chunk(body):
        lax.fori_loop(0, chunks, lambda c, carry: (body(c), carry)[1], 0)

    @each_chunk
    def _(c):
        for side in (0, 1):

            @pl.when(can_send(side))
            def _():
                w_copy(side, z, c, True).start()

    lse32[...] = lse_ref[0].astype(jnp.float32)
    delta32[...] = delta_ref[0].astype(jnp.float32)
    seg_row = seg_ref[:, pl.ds(pl.multiple_of(tok * window, LANES), window)].astype(jnp.float32)
    seg_col = jnp.transpose(jnp.broadcast_to(seg_row, (LANES, window)))[:, :1]
    key_id = lax.broadcasted_iota(jnp.int32, (window, window), 0)
    query_id = lax.broadcasted_iota(jnp.int32, (window, window), 1)
    bias[...] = jnp.where((seg_col == seg_row) & (key_id <= query_id), 0.0, -1e30)
    dk_acc[...] = jnp.zeros_like(dk_acc)
    dv_acc[...] = jnp.zeros_like(dv_acc)
    scale = head_size ** (-0.5)
    half = window // 2

    def dot(a, b, da, db):
        return lax.dot_general(a, b, (((da,), (db,)), ((), ())), preferred_element_type=jnp.float32)

    @pl.loop(0, groups)
    def _(r):
        cols = pl.ds(pl.multiple_of(r * head_size, head_size), head_size)
        pieces = []
        for first in (0, half):
            keys, queries = slice(first, first + half), slice(first, window)
            q, do = q_ref[queries, cols], do_ref[queries, cols]
            kk, vv = k_ref[keys, :], v_ref[keys, :]
            logits = dot(kk, q, 1, 1) * scale - lse32[pl.ds(r, 1), queries]
            probs = jnp.exp(logits + bias[keys, queries])
            dv_acc[keys, :] += dot(probs.astype(jnp.bfloat16), do, 1, 0)
            grad_prob = dot(vv, do, 1, 1)
            ds = (probs * (grad_prob - delta32[pl.ds(r, 1), queries])).astype(jnp.bfloat16)
            dk_acc[keys, :] += dot(ds, q, 1, 0)
            pieces.append(dot(ds, kk, 0, 0))
        low = pieces[0]
        joined[y, :half, cols] = (low[:half] * scale).astype(jnp.bfloat16)
        joined[y, half:, cols] = ((low[half:] + pieces[1]) * scale).astype(jnp.bfloat16)

    wide = groups * head_size
    joined[y, :, wide : wide + head_size] = (dk_acc[...] * scale).astype(jnp.bfloat16)
    joined[y, :, wide + head_size : wide + 2 * head_size] = dv_acc[...].astype(jnp.bfloat16)

    def p_copy(o, c, yd):
        return remote(
            part.at[o, c, yd], got.at[h, c, yd], p_send.at[o, c, yd], p_recv.at[h, c, yd], tok, o
        )

    def direct_copy(o, c, yd):
        return remote(
            part.at[o, c, yd],
            got.at[h, c, y],
            p_send.at[o, c, yd],
            p_recv.at[h, c, y],
            z * inner + yd,
            o,
        )

    def piece(o, c, yd, own):
        w = w_ref[own_w(c), :] if own else w_all[o, c]
        part[o, c, yd] = dot(joined[yd], w, 1, 1).astype(jnp.bfloat16)

    def send_piece(o, c, yd):
        @pl.when(o != h)
        def _():
            p_copy(o, c, yd).start()

    def arrive(side, s, c):
        o = z + s if side == 0 else z - s
        w_copy(side, o, c, False).wait_recv()

        @pl.when(can_send(side))
        def _():
            w_copy(side, o, c, False).start()

        return o

    def valid(side, s):
        return z + s < outer if side == 0 else z >= s

    def f_copy(c):
        return remote(fwd_out.at[c], fwd_in.at[c], f_send.at[c], f_recv.at[c], z * inner + yo, h)

    def total(c, yd):
        acc = part[h, c, yd].astype(jnp.float32)
        for step in range(1, heads):
            g = peer(step)
            remote(
                part.at[h, c, yd], got.at[g, c, yd], p_send.at[h, c, yd], p_recv.at[g, c, yd], tok, g
            ).wait_recv()
            acc += got[g, c, yd].astype(jnp.float32)
        return acc.astype(jnp.bfloat16)

    def out_cols(c, yd):
        return pl.ds(pl.multiple_of(yd * rows + c * LANES, LANES), LANES)

    def reduce_chunk(c):
        fwd_out[c] = total(c, yo)
        f_copy(c).start()
        out_ref[:, out_cols(c, y)] = total(c, y)

    distance = jnp.abs(z - h)
    j_copy = remote(joined.at[y], joined.at[y], j_send, j_recv, z * inner + yo, h)
    j_copy.start()

    @each_chunk
    def _(c):
        piece(z, c, y, True)
        send_piece(z, c, y)

    @each_chunk
    def _(c):
        for side in (0, 1):

            @pl.when(valid(side, 1))
            def _():
                o = arrive(side, 1, c)
                piece(o, c, y, False)
                send_piece(o, c, y)

    remote(joined.at[yo], joined.at[yo], j_send, j_recv, z * inner + yo, h).wait_recv()

    @each_chunk
    def _(c):
        piece(z, c, yo, True)
        send_piece(z, c, yo)
        for side in (0, 1):

            @pl.when(valid(side, 1))
            def _():
                o = z + 1 if side == 0 else z - 1
                piece(o, c, yo, False)
                send_piece(o, c, yo)

    @pl.when(distance == 0)
    def _():
        each_chunk(reduce_chunk)

    for s in range(2, outer):

        @each_chunk
        def _(c):
            for side in (0, 1):

                @pl.when(valid(side, s))
                def _():
                    o = arrive(side, s, c)
                    piece(o, c, yo, False)
                    piece(o, c, y, False)
                    if s < outer - 1:
                        send_piece(o, c, yo)
                        send_piece(o, c, y)
                    else:
                        direct_copy(o, c, yo).start()

                        @pl.when(o != h)
                        def _():
                            direct_copy(o, c, y).start()

            @pl.when(distance == s - 1)
            def _():
                reduce_chunk(c)

    def arrived(g, c, ys):
        remote(
            part.at[h, c, ys], got.at[g, c, ys], p_send.at[h, c, ys], p_recv.at[g, c, ys], tok, g
        ).wait_recv()
        return got[g, c, ys].astype(jnp.float32)

    @pl.when(distance == outer - 1)
    def _():
        @each_chunk
        def _(c):
            acc = part[h, c, y].astype(jnp.float32)
            for step in range(1, heads):
                acc += arrived(peer(step), c, y)
            out_ref[:, out_cols(c, y)] = acc.astype(jnp.bfloat16)
            other = arrived(h, c, yo)
            for step in range(1, heads):
                other += arrived(peer(step), c, yo)
            out_ref[:, out_cols(c, yo)] = other.astype(jnp.bfloat16)
            direct_copy(h, c, yo).wait_send()

    @pl.when(distance < outer - 1)
    def _():
        @each_chunk
        def _(c):
            f_copy(c).wait_recv()
            out_ref[:, out_cols(c, yo)] = fwd_in[c]
            f_copy(c).wait_send()

    j_copy.wait_send()

    @each_chunk
    def _(c):
        for step in range(1, heads):
            for yd in range(inner):
                p_copy(peer(step), c, yd).wait_send()
        for side in (0, 1):
            for s in range(outer):

                @pl.when(can_send(side) & valid(side, s))
                def _():
                    w_copy(side, z + s if side == 0 else z - s, c, s == 0).wait_send()


def fused(inner, outer, q, k, v, do, lse, delta, segments, weight):
    window, _, query_width = q.shape
    head_size = k.shape[2]
    rows, _, width = weight.shape
    chunks = rows // LANES
    bf16, f32 = jnp.bfloat16, jnp.float32
    dma = pltpu.SemaphoreType.DMA
    vmem = pl.BlockSpec(memory_space=pltpu.VMEM)
    return pl.pallas_call(
        functools.partial(fused_kernel, inner),
        out_shape=jax.ShapeDtypeStruct((window, inner * rows), bf16),
        in_specs=[vmem] * 8,
        out_specs=vmem,
        scratch_shapes=[
            pltpu.VMEM((inner, window, width), bf16),
            pltpu.VMEM((outer, chunks, LANES, width), bf16),
            pltpu.VMEM((outer, chunks, inner, window, LANES), bf16),
            pltpu.VMEM((outer, chunks, inner, window, LANES), bf16),
            pltpu.VMEM((chunks, window, LANES), bf16),
            pltpu.VMEM((chunks, window, LANES), bf16),
            pltpu.VMEM((window, window), f32),
            pltpu.VMEM(lse.shape[1:], f32),
            pltpu.VMEM(lse.shape[1:], f32),
            pltpu.VMEM((window, head_size), f32),
            pltpu.VMEM((window, head_size), f32),
            dma((2, outer, chunks)),
            dma((outer, chunks)),
            dma,
            dma,
            dma((outer, chunks, inner)),
            dma((outer, chunks, inner)),
            dma((chunks,)),
            dma((chunks,)),
        ],
        compiler_params=pltpu.CompilerParams(
            collective_id=0, has_side_effects=True, vmem_limit_bytes=60 * 1024 * 1024
        ),
    )(
        q.reshape(window, query_width),
        k.reshape(window, head_size),
        v.reshape(window, head_size),
        do.reshape(window, query_width),
        lse,
        delta,
        segments.reshape(1, -1),
        weight.reshape(rows, width),
    )


def solution(mesh):
    placed = (
        P("tok", "head", None),
        P("tok", "head", None),
        P("tok", "head", None),
        P("tok", "head", None),
        P("head", None, "tok"),
        P("head", None, "tok"),
        P(),
        P("tok", "head", None),
    )
    tok, heads = mesh.shape["tok"], mesh.shape["head"]

    def step(*args):
        window, kv_dev, _ = args[0].shape
        rows = args[7].shape[0]
        paired = tok == 2 * heads and heads > 2 and kv_dev == 1
        if paired and rows % LANES == 0 and window % (2 * LANES) == 0 and args[1].shape[2] == LANES:
            return fused(tok // heads, heads, *args)
        return on_device(*args)

    return jax.shard_map(
        step, mesh=mesh, in_specs=placed, out_specs=P("tok", "head"), check_vma=False
    )
```

profile of v0, /device:TPU:24, one launch (start us, length us, event | category | flops | bytes accessed | tf_op | source)
XLA Modules:
  0.0 107.8 jit_solution(10056471491472461458)
XLA Ops:
  0.0 105.5 %shard_map.82 = bf16[512,1024]{1,0:T(8,128)(2,1)} custom-call(bf16[512,1024]{1,0:T(8,128)(2,1)} %bitcast.7, bf16[512,128]{1,0:T(8,128)(2,1)} %bitcast.9, bf16[512,128]{1,0:T(8,128)(2,1)} %bitcast.10, bf16[512,1024]{1,0:T(8,128)(2,1)} %bitcast.8, bf16[1,8,512]{2,1,0:T(8,128)(2,1)} %lse_ref.1, bf16[1,8,512]{2,1,0:T(8,128)(2,1)} %delta_ref.1, ...), custom_call_target="tpu_custom_call" | custom-call | tf_op jit(solution)/shard_map/pallas_call | solution.py:432
  105.5 2.3 %copy.10 = bf16[512,1024]{1,0:T(8,128)(2,1)} copy(bf16[512,1024]{1,0:T(8,128)(2,1)} %shard_map.82) | data formatting | bytes 2097152
where the time goes:
time: 108 us
  Pallas kernels  105 us (97%)
  local copies, waits for them, and re-layouts  2.26 us (2%)
    pallas_call x1, Pallas kernels, fused(): pl.pallas_call(functools.partial(fused_kernel, inner), out_shape=jax.Shap...  105 us
    unnamed x1, local copies, waits for them, and re-layouts  2.26 us

commit v1 on v0

v1 whole, which is shorter than its diff:
```python
import functools

import jax
import jax.numpy as jnp
import numpy as np
from jax import lax
from jax.experimental import pallas as pl
from jax.experimental.pallas import tpu as pltpu
from jax.sharding import PartitionSpec as P

BLOCK = 128


def pair_lists(block_count):
    query_list = []
    key_list = []
    for query_block in range(block_count):
        for key_block in range(query_block + 1):
            query_list.append(query_block)
            key_list.append(key_block)
    return (np.array(query_list, np.int32), np.array(key_list, np.int32))


def live_pairs(seg_window, query_list, key_list, tile_rows):
    first_seg = jnp.take(seg_window, query_list * tile_rows)
    last_seg = jnp.take(seg_window, key_list * tile_rows + tile_rows - 1)
    return (first_seg == last_seg) | jnp.asarray(query_list == key_list)


def pair_grads(query_tile, dout_tile, key_tile, value_tile, lse_tile, delta_tile, allowed):
    tile_rows, groups, query_width = query_tile.shape
    head_size = key_tile.shape[2]
    heads_per_group = query_width // head_size
    query_heads = query_tile.reshape(tile_rows, groups, heads_per_group, head_size)
    dout_heads = dout_tile.reshape(tile_rows, groups, heads_per_group, head_size)
    scores = jnp.einsum(
        "agrd,bgd->grab", query_heads, key_tile, preferred_element_type=jnp.float32
    ) * head_size ** (-0.5)
    logits = scores - lse_tile.astype(jnp.float32)[:, :, :, None]
    soft_probs = jnp.where(allowed[None, None], jnp.exp(logits), 0.0)
    probs_low = soft_probs.astype(jnp.bfloat16)
    value_gradient = jnp.einsum(
        "grab,agrd->bgd", probs_low, dout_heads, preferred_element_type=jnp.float32
    )
    grad_prob = jnp.einsum(
        "agrd,bgd->grab", dout_heads, value_tile, preferred_element_type=jnp.float32
    )
    grad_score = (soft_probs * (grad_prob - delta_tile.astype(jnp.float32)[:, :, :, None])).astype(
        jnp.bfloat16
    )
    query_gradient = jnp.einsum(
        "grab,bgd->agrd", grad_score, key_tile, preferred_element_type=jnp.float32
    )
    key_gradient = jnp.einsum(
        "grab,agrd->bgd", grad_score, query_heads, preferred_element_type=jnp.float32
    )
    return (query_gradient.reshape(tile_rows, groups, query_width), key_gradient, value_gradient)


def on_device(
    query_rows,
    key_rows,
    value_rows,
    output_gradient,
    row_logsumexp,
    row_delta_sums,
    segments,
    query_key_value_weight,
):
    window, kv_dev, query_width = query_rows.shape
    head_size = key_rows.shape[2]
    tile_rows = BLOCK
    block_count = window // tile_rows
    query_list, key_list = pair_lists(block_count)
    query_table = jnp.asarray(query_list)
    key_table = jnp.asarray(key_list)
    myself = lax.axis_index("tok")
    own_seg = lax.dynamic_slice_in_dim(segments, myself * window, window)
    own_live = live_pairs(own_seg, query_list, key_list, tile_rows)
    block_ids = jnp.arange(block_count, dtype=jnp.int32)
    query_match = (query_table[:, None] == block_ids[None, :]) & own_live[:, None]
    key_match = key_table[:, None] == block_ids[None, :]
    block_local = jnp.any(query_match[:, :, None] & key_match[:, None, :], axis=0)
    token_local = jnp.repeat(jnp.repeat(block_local, tile_rows, axis=0), tile_rows, axis=1)
    offsets = jnp.arange(window, dtype=jnp.int32)
    allowed_all = (
        (own_seg[:, None] == own_seg[None, :])
        & (offsets[None, :] <= offsets[:, None])
        & token_local
    )
    local_out = pair_grads(
        query_rows,
        output_gradient,
        key_rows,
        value_rows,
        row_logsumexp,
        row_delta_sums,
        allowed_all,
    )
    acc_query = local_out[0].reshape(block_count, tile_rows, kv_dev, query_width)
    acc_key = local_out[1].reshape(block_count, tile_rows, kv_dev, head_size)
    acc_value = local_out[2].reshape(block_count, tile_rows, kv_dev, head_size)
    score_scale = head_size ** (-0.5)
    query_gradient = (acc_query * score_scale).reshape(window, kv_dev, query_width)
    key_gradient = (acc_key * score_scale).reshape(window, kv_dev, head_size)
    value_gradient = acc_value.reshape(window, kv_dev, head_size)
    stacked_gradients = (
        jnp.concatenate([query_gradient, key_gradient, value_gradient], axis=2)
        .astype(jnp.bfloat16)
        .reshape(window, -1)
    )
    weight_piece = lax.all_gather(query_key_value_weight, "tok", axis=0, tiled=True)
    flat_piece = weight_piece.reshape(weight_piece.shape[0], -1)
    partial_sum = lax.dot_general(
        stacked_gradients, flat_piece, (((1,), (1,)), ((), ())), preferred_element_type=jnp.float32
    )
    summed = lax.psum_scatter(
        partial_sum.astype(jnp.bfloat16), "head", scatter_dimension=1, tiled=True
    )
    return summed


MESH = pl.DeviceIdType.MESH
LANES = 128
PIECE = 32


def fused_kernel(
    sides,
    q_hbm,
    k_hbm,
    v_hbm,
    do_hbm,
    lse_ref,
    delta_ref,
    seg_ref,
    w_hbm,
    out_ref,
    q_ref,
    k_ref,
    v_ref,
    do_ref,
    joined,
    w_all,
    keep,
    part_out,
    part_in,
    x_out,
    x_in,
    back_out,
    back_in,
    bias,
    lse32,
    delta32,
    dk_acc,
    dv_acc,
    load_sem,
    own_send,
    own_recv,
    far_send,
    far_recv,
    relay_send,
    relay_recv,
    j_send,
    j_recv,
    part_send,
    part_recv,
    x_send,
    x_recv,
    back_send,
    back_recv,
):
    window, head_size = k_ref.shape
    groups = q_ref.shape[1] // head_size
    rows = w_hbm.shape[0]
    chunks, pieces = rows // LANES, rows // PIECE
    per = LANES // PIECE
    columns = groups + 2
    tok, h = lax.axis_index("tok"), lax.axis_index("head")
    z, y = tok // sides, tok % sides
    x, c = h // sides, h % sides
    yo, xo, co = 1 - y, 1 - x, 1 - c
    odd, upper = z % sides, z // sides
    partner = z + 1 - 2 * odd
    far = z + sides - 2 * sides * upper
    outer = upper == odd
    mine = jnp.where(c == odd, 0, 1)
    final = jnp.where(x == upper, 0, 1)

    def device(dz, dy, dx, dc):
        return (dz * sides + dy, dx * sides + dc)

    y_peer = device(z, yo, x, c)
    far_peer = device(far, y, x, c)
    j_peer = device(partner, y, x, c)
    core_peer = device(z, y, x, co)
    x_peer = device(z, y, xo, c)
    back_peer = device(partner, y, x, co)

    loads = [
        pltpu.make_async_copy(src, dst, load_sem.at[i])
        for i, (src, dst) in enumerate(
            (
                (k_hbm, k_ref),
                (v_hbm, v_ref),
                (q_hbm, q_ref),
                (do_hbm, do_ref),
                (w_hbm, w_all.at[0, y]),
            )
        )
    ]
    for load in loads:
        load.start()

    barrier = pltpu.get_barrier_semaphore()
    peers = (y_peer, far_peer, j_peer, core_peer, x_peer, back_peer)
    for peer in peers:
        pl.semaphore_signal(barrier, inc=1, device_id=peer, device_id_type=MESH)
    pl.semaphore_wait(barrier, len(peers))

    def remote(src, dst, send, recv, peer):
        return pltpu.make_async_remote_copy(
            src_ref=src,
            dst_ref=dst,
            send_sem=send,
            recv_sem=recv,
            device_id=peer,
            device_id_type=MESH,
        )

    def piece_rows(p):
        return pl.ds(pl.multiple_of(p * PIECE, PIECE), PIECE)

    def chunk_rows(k):
        return pl.ds(pl.multiple_of(k * LANES, LANES), LANES)

    def own_copy(p):
        return remote(
            w_hbm.at[piece_rows(p)],
            w_all.at[0, y, piece_rows(p)],
            own_send.at[p],
            own_recv.at[p],
            y_peer,
        )

    def far_copy(p):
        return remote(
            w_hbm.at[piece_rows(p)],
            w_all.at[1, y, piece_rows(p)],
            far_send.at[p],
            far_recv.at[p],
            far_peer,
        )

    def relay_copy(p):
        ref = w_all.at[1, y, piece_rows(p)]
        return remote(ref, ref, relay_send.at[p], relay_recv.at[p], y_peer)

    def arrived_own(p):
        ref = w_all.at[0, yo, piece_rows(p)]
        remote(ref, ref, own_send.at[p], own_recv.at[p], y_peer).wait_recv()

    def arrived_far(p):
        ref = w_all.at[1, y, piece_rows(p)]
        remote(ref, ref, far_send.at[p], far_recv.at[p], far_peer).wait_recv()

    def arrived_relay(p):
        ref = w_all.at[1, yo, piece_rows(p)]
        remote(ref, ref, relay_send.at[p], relay_recv.at[p], y_peer).wait_recv()

    def j_cols(r):
        return pl.ds(pl.multiple_of(r * head_size, head_size), head_size)

    def j_copy(r):
        return remote(
            joined.at[0, :, j_cols(r)],
            joined.at[1, :, j_cols(r)],
            j_send.at[r],
            j_recv.at[r],
            j_peer,
        )

    def each(count, body):
        lax.fori_loop(0, count, lambda i, carry: (body(i), carry)[1], 0)

    first = 2

    each(pieces, lambda p: own_copy(p).start())

    @pl.when(outer)
    def _():
        each(first, lambda p: far_copy(p).start())

    @pl.when(jnp.logical_not(outer))
    def _():
        each(pieces, lambda p: far_copy(p).start())

    lse32[...] = lse_ref[0].astype(jnp.float32)
    delta32[...] = delta_ref[0].astype(jnp.float32)
    seg_row = seg_ref[:, pl.ds(pl.multiple_of(tok * window, LANES), window)].astype(jnp.float32)
    seg_col = jnp.transpose(jnp.broadcast_to(seg_row, (LANES, window)))[:, :1]
    key_id = lax.broadcasted_iota(jnp.int32, (window, window), 0)
    query_id = lax.broadcasted_iota(jnp.int32, (window, window), 1)
    bias[...] = jnp.where((seg_col == seg_row) & (key_id <= query_id), 0.0, -1e30)
    dk_acc[...] = jnp.zeros_like(dk_acc)
    dv_acc[...] = jnp.zeros_like(dv_acc)
    scale = head_size ** (-0.5)
    half = window // 2

    def dot(a, b, da, db):
        return lax.dot_general(a, b, (((da,), (db,)), ((), ())), preferred_element_type=jnp.float32)

    for load in loads[:4]:
        load.wait()

    @pl.loop(0, groups)
    def _(r):
        cols = j_cols(r)
        sums = []
        for start in (0, half):
            keys, queries = slice(start, start + half), slice(start, window)
            q, do = q_ref[queries, cols], do_ref[queries, cols]
            kk, vv = k_ref[keys, :], v_ref[keys, :]
            logits = dot(kk, q, 1, 1) * scale - lse32[pl.ds(r, 1), queries]
            probs = jnp.exp(logits + bias[keys, queries])
            dv_acc[keys, :] += dot(probs.astype(jnp.bfloat16), do, 1, 0)
            grad_prob = dot(vv, do, 1, 1)
            ds = (probs * (grad_prob - delta32[pl.ds(r, 1), queries])).astype(jnp.bfloat16)
            dk_acc[keys, :] += dot(ds, q, 1, 0)
            sums.append(dot(ds, kk, 0, 0))
        low = sums[0]
        joined[0, :half, cols] = (low[:half] * scale).astype(jnp.bfloat16)
        joined[0, half:, cols] = ((low[half:] + sums[1]) * scale).astype(jnp.bfloat16)

        @pl.when(outer)
        def _():
            j_copy(r).start()

    wide = groups * head_size
    joined[0, :, wide : wide + head_size] = (dk_acc[...] * scale).astype(jnp.bfloat16)
    joined[0, :, wide + head_size : wide + 2 * head_size] = dv_acc[...].astype(jnp.bfloat16)
    loads[4].wait()

    def part_copy(slot, yr, k):
        return remote(
            part_out.at[slot, yr, k],
            part_in.at[slot, yr, k],
            part_send.at[slot, yr, k],
            part_recv.at[slot, yr, k],
            core_peer,
        )

    def x_copy(yr, k):
        return remote(
            x_out.at[yr, k], x_in.at[yr, k], x_send.at[yr, k], x_recv.at[yr, k], x_peer
        )

    def back_copy(yr, k):
        return remote(
            back_out.at[yr, k], back_in.at[yr, k], back_send.at[yr, k], back_recv.at[yr, k], back_peer
        )

    def unit(slot, yr, k, side):
        value = dot(joined[side], w_all[slot, yr, chunk_rows(k)], 1, 1)

        @pl.when(mine == side)
        def _():
            keep[slot, yr, k] = value

        @pl.when(mine != side)
        def _():
            part_out[slot, yr, k] = value.astype(jnp.bfloat16)
            part_copy(slot, yr, k).start()

    def core_sum(slot, yr, k):
        part_copy(slot, yr, k).wait_recv()
        value = keep[slot, yr, k] + part_in[slot, yr, k].astype(jnp.float32)

        @pl.when(slot == final)
        def _():
            keep[slot, yr, k] = value

        @pl.when(slot != final)
        def _():
            x_out[yr, k] = value.astype(jnp.bfloat16)
            x_copy(yr, k).start()

    def out_cols(yr, k):
        return pl.ds(pl.multiple_of(yr * rows + k * LANES, LANES), LANES)

    def x_sum(yr, k):
        x_copy(yr, k).wait_recv()
        value = (keep[final, yr, k] + x_in[yr, k].astype(jnp.float32)).astype(jnp.bfloat16)

        @pl.when(mine == 0)
        def _():
            out_ref[:, out_cols(yr, k)] = value

        @pl.when(mine == 1)
        def _():
            back_out[yr, k] = value
            back_copy(yr, k).start()

    def wait_chunk(arrived, k):
        for i in range(per):
            arrived(k * per + i)

    def which(i):
        return jnp.where(i // chunks % 2 == 0, y, yo)

    lag = 2

    @pl.when(outer)
    def _():
        j_copy(groups).start()
        j_copy(groups + 1).start()
        each(pieces - first, lambda p: far_copy(p + first).start())
        steps = 4 * chunks
        share = 2 * pieces // steps

        @pl.loop(0, steps + lag)
        def _(i):
            k = i % chunks

            @pl.when(i < steps // 2)
            def _():
                for j in range(share):
                    arrived_far(i * share + j)
                    relay_copy(i * share + j).start()

            @pl.when((i >= chunks) & (i < 2 * chunks))
            def _():
                wait_chunk(arrived_own, k)

            @pl.when((i >= 3 * chunks) & (i < steps))
            def _():
                wait_chunk(arrived_relay, k)

            @pl.when(i < steps)
            def _():
                unit(i // (2 * chunks), which(i), k, 0)

            @pl.when((i >= lag) & (mine == 0))
            def _():
                core_sum((i - lag) // (2 * chunks), which(i - lag), (i - lag) % chunks)

        @pl.when(mine == 0)
        def _():
            each(2 * chunks, lambda i: x_sum(which(i), i % chunks))

        each(columns, lambda r: j_copy(r).wait_recv())

        @pl.loop(0, chunks + 2)
        def _(k):
            @pl.when(k < chunks)
            def _():
                for slot in (0, 1):
                    for yr in (y, yo):
                        unit(slot, yr, k, 1)

            @pl.when((k >= 1) & (k <= chunks) & (mine == 1))
            def _():
                for slot in (0, 1):
                    for yr in (y, yo):
                        core_sum(slot, yr, k - 1)

            @pl.when((k >= 2) & (mine == 1))
            def _():
                for yr in (y, yo):
                    x_sum(yr, k - 2)

    @pl.when(jnp.logical_not(outer))
    def _():
        @pl.loop(0, 2 * chunks + lag)
        def _(i):
            k = i % chunks

            @pl.when(i == 2 * chunks - 1)
            def _():
                each(columns, lambda r: j_copy(r).start())

            @pl.when((i >= chunks) & (i < 2 * chunks))
            def _():
                wait_chunk(arrived_own, k)

            @pl.when(i < 2 * chunks)
            def _():
                unit(0, which(i), k, 0)

            @pl.when((i >= lag) & (mine == 0))
            def _():
                core_sum(0, which(i - lag), (i - lag) % chunks)

        each(columns, lambda r: j_copy(r).wait_recv())

        @pl.loop(0, 2 * chunks + lag)
        def _(i):
            @pl.when(i < 2 * chunks)
            def _():
                unit(0, which(i), i % chunks, 1)

            @pl.when((i >= lag) & (mine == 1))
            def _():
                core_sum(0, which(i - lag), (i - lag) % chunks)

        @pl.loop(0, chunks + 2)
        def _(k):
            for i in range(per):

                @pl.when(k < chunks)
                def _():
                    arrived_far(k * per + i)
                    relay_copy(k * per + i).start()

                @pl.when((k >= 1) & (k <= chunks))
                def _():
                    if i == 0:
                        unit(1, y, k - 1, 0)
                        unit(1, y, k - 1, 1)
                    if i == 1:
                        wait_chunk(arrived_relay, k - 1)
                        unit(1, yo, k - 1, 0)
                        unit(1, yo, k - 1, 1)
                    if i == 2:
                        core_sum(1, y, k - 1)
                        core_sum(1, yo, k - 1)

                @pl.when(k >= 2)
                def _():
                    if i == 3:
                        x_sum(y, k - 2)
                        x_sum(yo, k - 2)

    @pl.when(mine == 1)
    def _():
        @pl.loop(0, 2 * chunks)
        def _(i):
            k, yr = i // 2, jnp.where(i % 2 == 0, y, yo)
            back_copy(yr, k).wait_recv()
            out_ref[:, out_cols(yr, k)] = back_in[yr, k]
            back_copy(yr, k).wait_send()

    @pl.loop(0, pieces)
    def _(p):
        own_copy(p).wait_send()
        far_copy(p).wait_send()
        relay_copy(p).wait_send()

    each(columns, lambda r: j_copy(r).wait_send())

    @pl.loop(0, 2 * chunks)
    def _(i):
        yr, k = i // chunks, i % chunks
        part_copy(0, yr, k).wait_send()
        part_copy(1, yr, k).wait_send()
        x_copy(yr, k).wait_send()


def fused(sides, q, k, v, do, lse, delta, segments, weight):
    window, _, query_width = q.shape
    head_size = k.shape[2]
    rows, _, width = weight.shape
    chunks, pieces = rows // LANES, rows // PIECE
    columns = width // head_size
    bf16, f32 = jnp.bfloat16, jnp.float32
    dma = pltpu.SemaphoreType.DMA
    vmem = pl.BlockSpec(memory_space=pltpu.VMEM)
    hbm = pl.BlockSpec(memory_space=pl.ANY)
    tile = (window, LANES)
    return pl.pallas_call(
        functools.partial(fused_kernel, sides),
        out_shape=jax.ShapeDtypeStruct((window, 2 * rows), bf16),
        in_specs=[hbm] * 4 + [vmem] * 3 + [hbm],
        out_specs=vmem,
        scratch_shapes=[
            pltpu.VMEM((window, query_width), bf16),
            pltpu.VMEM((window, head_size), bf16),
            pltpu.VMEM((window, head_size), bf16),
            pltpu.VMEM((window, query_width), bf16),
            pltpu.VMEM((2, window, width), bf16),
            pltpu.VMEM((2, 2, rows, width), bf16),
            pltpu.VMEM((2, 2, chunks) + tile, f32),
            pltpu.VMEM((2, 2, chunks) + tile, bf16),
            pltpu.VMEM((2, 2, chunks) + tile, bf16),
            pltpu.VMEM((2, chunks) + tile, bf16),
            pltpu.VMEM((2, chunks) + tile, bf16),
            pltpu.VMEM((2, chunks) + tile, bf16),
            pltpu.VMEM((2, chunks) + tile, bf16),
            pltpu.VMEM((window, window), f32),
            pltpu.VMEM(lse.shape[1:], f32),
            pltpu.VMEM(lse.shape[1:], f32),
            pltpu.VMEM((window, head_size), f32),
            pltpu.VMEM((window, head_size), f32),
            dma((5,)),
            dma((pieces,)),
            dma((pieces,)),
            dma((pieces,)),
            dma((pieces,)),
            dma((pieces,)),
            dma((pieces,)),
            dma((columns,)),
            dma((columns,)),
            dma((2, 2, chunks)),
            dma((2, 2, chunks)),
            dma((2, chunks)),
            dma((2, chunks)),
            dma((2, chunks)),
            dma((2, chunks)),
        ],
        compiler_params=pltpu.CompilerParams(
            collective_id=0, has_side_effects=True, vmem_limit_bytes=60 * 1024 * 1024
        ),
    )(
        q.reshape(window, query_width),
        k.reshape(window, head_size),
        v.reshape(window, head_size),
        do.reshape(window, query_width),
        lse,
        delta,
        segments.reshape(1, -1),
        weight.reshape(rows, width),
    )


def solution(mesh):
    placed = (
        P("tok", "head", None),
        P("tok", "head", None),
        P("tok", "head", None),
        P("tok", "head", None),
        P("head", None, "tok"),
        P("head", None, "tok"),
        P(),
        P("tok", "head", None),
    )
    tok, heads = mesh.shape["tok"], mesh.shape["head"]
    sides = tok // heads

    def step(*args):
        window, kv_dev, _ = args[0].shape
        rows = args[7].shape[0]
        paired = sides == 2 and heads == sides * sides and tok == heads * sides and kv_dev == 1
        if paired and rows % LANES == 0 and window % (2 * LANES) == 0 and args[1].shape[2] == LANES:
            return fused(sides, *args)
        return on_device(*args)

    return jax.shard_map(
        step, mesh=mesh, in_specs=placed, out_specs=P("tok", "head"), check_vma=False
    )
```

time: 108 us -> 97.8 us (0.906)
  the two profiles are of different devices: /device:TPU:24 before, /device:TPU:17 now
where the time goes in v1:
time: 97.8 us; the launch traced here: 97.5 us
  Pallas kernels  95.2 us (97%)
  local copies, waits for them, and re-layouts  2.26 us (2%)
    pallas_call x1, Pallas kernels, fused(): pl.pallas_call(functools.partial(fused_kernel, sides), out_shape=jax.Shap...  95.2 us
    unnamed x1, local copies, waits for them, and re-layouts  2.26 us

profile of v1, /device:TPU:17, one launch (start us, length us, event | category | flops | bytes accessed | tf_op | source)
XLA Modules:
  0.0 97.5 jit_solution(289242984899453344)
XLA Ops:
  0.0 95.2 %shard_map.82 = bf16[512,1024]{1,0:T(8,128)(2,1)} custom-call(bf16[512,1024]{1,0:T(8,128)(2,1)} %bitcast.7, bf16[512,128]{1,0:T(8,128)(2,1)} %bitcast.9, bf16[512,128]{1,0:T(8,128)(2,1)} %bitcast.10, bf16[512,1024]{1,0:T(8,128)(2,1)} %bitcast.8, bf16[1,8,512]{2,1,0:T(8,128)(2,1)} %lse_ref.1, bf16[1,8,512]{2,1,0:T(8,128)(2,1)} %delta_ref.1, ...), custom_call_target="tpu_custom_call" | custom-call | tf_op jit(solution)/shard_map/pallas_call | solution.py:570
  95.2 2.3 %copy.10 = bf16[512,1024]{1,0:T(8,128)(2,1)} copy(bf16[512,1024]{1,0:T(8,128)(2,1)} %shard_map.82) | data formatting | bytes 2097152

commit v2 on v1

--- a/solution.py
+++ b/solution.py
@@ -148,7 +148,6 @@
     x_out,
     x_in,
     back_out,
-    back_in,
     bias,
     lse32,
     delta32,
@@ -175,6 +174,7 @@
     rows = w_hbm.shape[0]
     chunks, pieces = rows // LANES, rows // PIECE
     per = LANES // PIECE
+    block = window // chunks
     columns = groups + 2
     tok, h = lax.axis_index("tok"), lax.axis_index("head")
     z, y = tok // sides, tok % sides
@@ -234,6 +234,9 @@
     def chunk_rows(k):
         return pl.ds(pl.multiple_of(k * LANES, LANES), LANES)
 
+    def block_rows(i):
+        return pl.ds(pl.multiple_of(i * block, block), block)
+
     def own_copy(p):
         return remote(
             w_hbm.at[piece_rows(p)],
@@ -277,6 +280,15 @@
             joined.at[1, :, j_cols(r)],
             j_send.at[r],
             j_recv.at[r],
+            j_peer,
+        )
+
+    def j_block(i):
+        return remote(
+            joined.at[0, block_rows(i)],
+            joined.at[1, block_rows(i)],
+            j_send.at[i],
+            j_recv.at[i],
             j_peer,
         )
 
@@ -341,23 +353,42 @@
     joined[0, :, wide + head_size : wide + 2 * head_size] = dv_acc[...].astype(jnp.bfloat16)
     loads[4].wait()
 
-    def part_copy(slot, yr, k):
+    def tile(ref, lead, i, by_token):
+        return ref.at[(*lead, slice(None), block_rows(i))] if by_token else ref.at[(*lead, i)]
+
+    def part_copy(slot, yr, i, by_token):
         return remote(
-            part_out.at[slot, yr, k],
-            part_in.at[slot, yr, k],
-            part_send.at[slot, yr, k],
-            part_recv.at[slot, yr, k],
+            tile(part_out, (slot, yr), i, by_token),
+            tile(part_in, (slot, yr), i, by_token),
+            part_send.at[slot, yr, i],
+            part_recv.at[slot, yr, i],
             core_peer,
         )
 
-    def x_copy(yr, k):
+    def x_copy(yr, i, by_token):
         return remote(
-            x_out.at[yr, k], x_in.at[yr, k], x_send.at[yr, k], x_recv.at[yr, k], x_peer
-        )
-
-    def back_copy(yr, k):
+            tile(x_out, (yr,), i, by_token),
+            tile(x_in, (yr,), i, by_token),
+            x_send.at[yr, i],
+            x_recv.at[yr, i],
+            x_peer,
+        )
+
+    def out_cols(yr, k):
+        return pl.ds(pl.multiple_of(yr * rows + k * LANES, LANES), LANES)
+
+    def out_tile(ref, yr, i, by_token):
+        if by_token:
+            return ref.at[block_rows(i), pl.ds(pl.multiple_of(yr * rows, LANES), rows)]
+        return ref.at[:, out_cols(yr, i)]
+
+    def back_copy(yr, i, by_token):
         return remote(
-            back_out.at[yr, k], back_in.at[yr, k], back_send.at[yr, k], back_recv.at[yr, k], back_peer
+            out_tile(back_out, yr, i, by_token),
+            out_tile(out_ref, yr, i, by_token),
+            back_send.at[yr, i],
+            back_recv.at[yr, i],
+            back_peer,
         )
 
     def unit(slot, yr, k, side):
@@ -370,36 +401,63 @@
         @pl.when(mine != side)
         def _():
             part_out[slot, yr, k] = value.astype(jnp.bfloat16)
-            part_copy(slot, yr, k).start()
-
-    def core_sum(slot, yr, k):
-        part_copy(slot, yr, k).wait_recv()
-        value = keep[slot, yr, k] + part_in[slot, yr, k].astype(jnp.float32)
+            part_copy(slot, yr, k, False).start()
+
+    def block_unit(slot, yr, i):
+        value = dot(joined[1, block_rows(i)], w_all[slot, yr], 1, 1)
+
+        @pl.when(mine == 1)
+        def _():
+            for k in range(chunks):
+                keep[slot, yr, k, block_rows(i)] = value[:, k * LANES : (k + 1) * LANES]
+
+        @pl.when(mine == 0)
+        def _():
+            low = value.astype(jnp.bfloat16)
+            for k in range(chunks):
+                part_out[slot, yr, k, block_rows(i)] = low[:, k * LANES : (k + 1) * LANES]
+            part_copy(slot, yr, i, True).start()
+
+    def core_sum(slot, yr, i, by_token):
+        part_copy(slot, yr, i, by_token).wait_recv()
+        kept = tile(keep, (slot, yr), i, by_token)
+        value = kept[...] + tile(part_in, (slot, yr), i, by_token)[...].astype(jnp.float32)
 
         @pl.when(slot == final)
         def _():
-            keep[slot, yr, k] = value
+            kept[...] = value
 
         @pl.when(slot != final)
         def _():
-            x_out[yr, k] = value.astype(jnp.bfloat16)
-            x_copy(yr, k).start()
-
-    def out_cols(yr, k):
-        return pl.ds(pl.multiple_of(yr * rows + k * LANES, LANES), LANES)
-
-    def x_sum(yr, k):
-        x_copy(yr, k).wait_recv()
-        value = (keep[final, yr, k] + x_in[yr, k].astype(jnp.float32)).astype(jnp.bfloat16)
-
-        @pl.when(mine == 0)
-        def _():
-            out_ref[:, out_cols(yr, k)] = value
-
-        @pl.when(mine == 1)
-        def _():
-            back_out[yr, k] = value
-            back_copy(yr, k).start()
+            tile(x_out, (yr,), i, by_token)[...] = value.astype(jnp.bfloat16)
+            x_copy(yr, i, by_token).start()
+
+    def x_sum(yr, i, by_token):
+        x_copy(yr, i, by_token).wait_recv()
+        value = tile(keep, (final, yr), i, by_token)[...]
+        value += tile(x_in, (yr,), i, by_token)[...].astype(jnp.float32)
+        value = value.astype(jnp.bfloat16)
+
+        def put(ref):
+            if by_token:
+                for k in range(chunks):
+                    ref[block_rows(i), out_cols(yr, k)] = value[k]
+            else:
+                ref[:, out_cols(yr, i)] = value
+
+        if by_token:
+            put(back_out)
+            back_copy(yr, i, True).start()
+        else:
+
+            @pl.when(mine == 0)
+            def _():
+                put(out_ref)
+
+            @pl.when(mine == 1)
+            def _():
+                put(back_out)
+                back_copy(yr, i, False).start()
 
     def wait_chunk(arrived, k):
         for i in range(per):
@@ -415,14 +473,14 @@
         j_copy(groups).start()
         j_copy(groups + 1).start()
         each(pieces - first, lambda p: far_copy(p + first).start())
-        steps = 4 * chunks
-        share = 2 * pieces // steps
+        steps = 3 * chunks
+        share = pieces // (2 * chunks)
 
         @pl.loop(0, steps + lag)
         def _(i):
             k = i % chunks
 
-            @pl.when(i < steps // 2)
+            @pl.when(i < 2 * chunks)
             def _():
                 for j in range(share):
                     arrived_far(i * share + j)
@@ -432,42 +490,62 @@
             def _():
                 wait_chunk(arrived_own, k)
 
-            @pl.when((i >= 3 * chunks) & (i < steps))
-            def _():
-                wait_chunk(arrived_relay, k)
-
             @pl.when(i < steps)
             def _():
                 unit(i // (2 * chunks), which(i), k, 0)
 
             @pl.when((i >= lag) & (mine == 0))
             def _():
-                core_sum((i - lag) // (2 * chunks), which(i - lag), (i - lag) % chunks)
-
-        @pl.when(mine == 0)
+                core_sum((i - lag) // (2 * chunks), which(i - lag), (i - lag) % chunks, False)
+
+        @pl.loop(0, chunks + 2)
+        def _(i):
+            @pl.when(i < chunks)
+            def _():
+                wait_chunk(arrived_relay, i)
+                unit(1, yo, i, 0)
+                j_block(i).wait_recv()
+                block_unit(0, y, i)
+                block_unit(0, yo, i)
+                block_unit(1, y, i)
+
+            @pl.when(i == chunks)
+            def _():
+                each(chunks, lambda j: block_unit(1, yo, j))
+
+            @pl.when(mine == 0)
+            def _():
+                @pl.when((i >= 1) & (i <= chunks))
+                def _():
+                    core_sum(1, yo, i - 1, False)
+                    x_sum(y, i - 1, False)
+
+                @pl.when(i >= 2)
+                def _():
+                    x_sum(yo, i - 2, False)
+
+            @pl.when(mine == 1)
+            def _():
+                @pl.when((i >= 1) & (i <= chunks))
+                def _():
+                    for slot, yr in ((0, y), (0, yo), (1, y)):
+                        core_sum(slot, yr, i - 1, True)
+
+                @pl.when(i == chunks + 1)
+                def _():
+                    each(chunks, lambda j: core_sum(1, yo, j, True))
+
+                @pl.when(i >= 2)
+                def _():
+                    x_sum(y, i - 2, True)
+
+                @pl.when((i >= 2) & (final == 0))
+                def _():
+                    x_sum(yo, i - 2, True)
+
+        @pl.when((mine == 1) & (final == 1))
         def _():
-            each(2 * chunks, lambda i: x_sum(which(i), i % chunks))
-
-        each(columns, lambda r: j_copy(r).wait_recv())
-
-        @pl.loop(0, chunks + 2)
-        def _(k):
-            @pl.when(k < chunks)
-            def _():
-                for slot in (0, 1):
-                    for yr in (y, yo):
-                        unit(slot, yr, k, 1)
-
-            @pl.when((k >= 1) & (k <= chunks) & (mine == 1))
-            def _():
-                for slot in (0, 1):
-                    for yr in (y, yo):
-                        core_sum(slot, yr, k - 1)
-
-            @pl.when((k >= 2) & (mine == 1))
-            def _():
-                for yr in (y, yo):
-                    x_sum(yr, k - 2)
+            each(chunks, lambda j: x_sum(yo, j, True))
 
     @pl.when(jnp.logical_not(outer))
     def _():
@@ -477,7 +555,7 @@
 
             @pl.when(i == 2 * chunks - 1)
             def _():
-                each(columns, lambda r: j_copy(r).start())
+                each(chunks, lambda j: j_block(j).start())
 
             @pl.when((i >= chunks) & (i < 2 * chunks))
             def _():
@@ -489,19 +567,9 @@
 
             @pl.when((i >= lag) & (mine == 0))
             def _():
-                core_sum(0, which(i - lag), (i - lag) % chunks)
+                core_sum(0, which(i - lag), (i - lag) % chunks, False)
 
         each(columns, lambda r: j_copy(r).wait_recv())
-
-        @pl.loop(0, 2 * chunks + lag)
-        def _(i):
-            @pl.when(i < 2 * chunks)
-            def _():
-                unit(0, which(i), i % chunks, 1)
-
-            @pl.when((i >= lag) & (mine == 1))
-            def _():
-                core_sum(0, which(i - lag), (i - lag) % chunks)
 
         @pl.loop(0, chunks + 2)
         def _(k):
@@ -512,33 +580,44 @@
                     arrived_far(k * per + i)
                     relay_copy(k * per + i).start()
 
+                @pl.when(k == 0)
+                def _():
+                    for j in range(i * 2 * chunks // per, (i + 1) * 2 * chunks // per):
+                        unit(0, which(j), j % chunks, 1)
+
+                @pl.when((k == 1) & (mine == 1))
+                def _():
+                    for j in range(i * 2 * chunks // per, (i + 1) * 2 * chunks // per):
+                        core_sum(0, which(j), j % chunks, False)
+
                 @pl.when((k >= 1) & (k <= chunks))
                 def _():
                     if i == 0:
                         unit(1, y, k - 1, 0)
+                    if i == 1:
                         unit(1, y, k - 1, 1)
-                    if i == 1:
+                    if i == 2:
                         wait_chunk(arrived_relay, k - 1)
                         unit(1, yo, k - 1, 0)
+                        core_sum(1, y, k - 1, False)
+                    if i == 3:
                         unit(1, yo, k - 1, 1)
-                    if i == 2:
-                        core_sum(1, y, k - 1)
-                        core_sum(1, yo, k - 1)
 
                 @pl.when(k >= 2)
                 def _():
+                    if i == 0:
+                        core_sum(1, yo, k - 2, False)
+                    if i == 1:
+                        x_sum(y, k - 2, False)
                     if i == 3:
-                        x_sum(y, k - 2)
-                        x_sum(yo, k - 2)
+                        x_sum(yo, k - 2, False)
 
     @pl.when(mine == 1)
     def _():
         @pl.loop(0, 2 * chunks)
         def _(i):
-            k, yr = i // 2, jnp.where(i % 2 == 0, y, yo)
-            back_copy(yr, k).wait_recv()
-            out_ref[:, out_cols(yr, k)] = back_in[yr, k]
-            back_copy(yr, k).wait_send()
+            back_copy(i // chunks, i % chunks, False).wait_recv()
+            back_copy(i // chunks, i % chunks, False).wait_send()
 
     @pl.loop(0, pieces)
     def _(p):
@@ -546,14 +625,20 @@
         far_copy(p).wait_send()
         relay_copy(p).wait_send()
 
-    each(columns, lambda r: j_copy(r).wait_send())
+    @pl.when(outer)
+    def _():
+        each(columns, lambda r: j_copy(r).wait_send())
+
+    @pl.when(jnp.logical_not(outer))
+    def _():
+        each(chunks, lambda i: j_block(i).wait_send())
 
     @pl.loop(0, 2 * chunks)
     def _(i):
         yr, k = i // chunks, i % chunks
-        part_copy(0, yr, k).wait_send()
-        part_copy(1, yr, k).wait_send()
-        x_copy(yr, k).wait_send()
+        part_copy(0, yr, k, False).wait_send()
+        part_copy(1, yr, k, False).wait_send()
+        x_copy(yr, k, False).wait_send()
 
 
 def fused(sides, q, k, v, do, lse, delta, segments, weight):
@@ -584,8 +669,7 @@
             pltpu.VMEM((2, 2, chunks) + tile, bf16),
             pltpu.VMEM((2, chunks) + tile, bf16),
             pltpu.VMEM((2, chunks) + tile, bf16),
-            pltpu.VMEM((2, chunks) + tile, bf16),
-            pltpu.VMEM((2, chunks) + tile, bf16),
+            pltpu.VMEM((window, 2 * rows), bf16),
             pltpu.VMEM((window, window), f32),
             pltpu.VMEM(lse.shape[1:], f32),
             pltpu.VMEM(lse.shape[1:], f32),

time: 97.8 us -> 89.7 us (0.917)
  Pallas kernels: 95.2 us -> 87.1 us
    pallas_call x1, Pallas kernels: 95.2 us -> 87.1 us  [fused(): pl.pallas_call(functools.partial(fused_kernel, sides), out_shape=jax.Shap...]
where the time goes in v2:
time: 89.7 us; the launch traced here: 89.4 us
  Pallas kernels  87.1 us (97%)
  local copies, waits for them, and re-layouts  2.26 us (3%)
    pallas_call x1, Pallas kernels, fused(): pl.pallas_call(functools.partial(fused_kernel, sides), out_shape=jax.Shap...  87.1 us
    unnamed x1, local copies, waits for them, and re-layouts  2.26 us

profile of v2, /device:TPU:17, one launch (start us, length us, event | category | flops | bytes accessed | tf_op | source)
XLA Modules:
  0.0 89.4 jit_solution(3924614660940371576)
XLA Ops:
  0.0 87.1 %shard_map.82 = bf16[512,1024]{1,0:T(8,128)(2,1)} custom-call(bf16[512,1024]{1,0:T(8,128)(2,1)} %bitcast.7, bf16[512,128]{1,0:T(8,128)(2,1)} %bitcast.9, bf16[512,128]{1,0:T(8,128)(2,1)} %bitcast.10, bf16[512,1024]{1,0:T(8,128)(2,1)} %bitcast.8, bf16[1,8,512]{2,1,0:T(8,128)(2,1)} %lse_ref.1, bf16[1,8,512]{2,1,0:T(8,128)(2,1)} %delta_ref.1, ...), custom_call_target="tpu_custom_call" | custom-call | tf_op jit(solution)/shard_map/pallas_call | solution.py:655
  87.1 2.3 %copy.10 = bf16[512,1024]{1,0:T(8,128)(2,1)} copy(bf16[512,1024]{1,0:T(8,128)(2,1)} %shard_map.82) | data formatting | bytes 2097152

commit v3 on v2

--- a/solution.py
+++ b/solution.py
@@ -131,15 +131,18 @@
     k_hbm,
     v_hbm,
     do_hbm,
-    lse_ref,
-    delta_ref,
-    seg_ref,
+    lse_hbm,
+    delta_hbm,
+    seg_hbm,
     w_hbm,
     out_ref,
     q_ref,
     k_ref,
     v_ref,
     do_ref,
+    lse_ref,
+    delta_ref,
+    seg_ref,
     joined,
     w_all,
     keep,
@@ -201,6 +204,9 @@
         pltpu.make_async_copy(src, dst, load_sem.at[i])
         for i, (src, dst) in enumerate(
             (
+                (seg_hbm, seg_ref),
+                (lse_hbm, lse_ref),
+                (delta_hbm, delta_ref),
                 (k_hbm, k_ref),
                 (v_hbm, v_ref),
                 (q_hbm, q_ref),
@@ -307,8 +313,10 @@
     def _():
         each(pieces, lambda p: far_copy(p).start())
 
-    lse32[...] = lse_ref[0].astype(jnp.float32)
-    delta32[...] = delta_ref[0].astype(jnp.float32)
+    for load in loads[:3]:
+        load.wait()
+    lse32[...] = lse_ref[...].astype(jnp.float32)
+    delta32[...] = delta_ref[...].astype(jnp.float32)
     seg_row = seg_ref[:, pl.ds(pl.multiple_of(tok * window, LANES), window)].astype(jnp.float32)
     seg_col = jnp.transpose(jnp.broadcast_to(seg_row, (LANES, window)))[:, :1]
     key_id = lax.broadcasted_iota(jnp.int32, (window, window), 0)
@@ -322,7 +330,7 @@
     def dot(a, b, da, db):
         return lax.dot_general(a, b, (((da,), (db,)), ((), ())), preferred_element_type=jnp.float32)
 
-    for load in loads[:4]:
+    for load in loads[3:7]:
         load.wait()
 
     @pl.loop(0, groups)
@@ -351,7 +359,7 @@
     wide = groups * head_size
     joined[0, :, wide : wide + head_size] = (dk_acc[...] * scale).astype(jnp.bfloat16)
     joined[0, :, wide + head_size : wide + 2 * head_size] = dv_acc[...].astype(jnp.bfloat16)
-    loads[4].wait()
+    loads[7].wait()
 
     def tile(ref, lead, i, by_token):
         return ref.at[(*lead, slice(None), block_rows(i))] if by_token else ref.at[(*lead, i)]
@@ -498,7 +506,7 @@
             def _():
                 core_sum((i - lag) // (2 * chunks), which(i - lag), (i - lag) % chunks, False)
 
-        @pl.loop(0, chunks + 2)
+        @pl.loop(0, chunks + 1)
         def _(i):
             @pl.when(i < chunks)
             def _():
@@ -509,39 +517,39 @@
                 block_unit(0, yo, i)
                 block_unit(1, y, i)
 
-            @pl.when(i == chunks)
+            @pl.when(i == chunks - 1)
             def _():
                 each(chunks, lambda j: block_unit(1, yo, j))
 
             @pl.when(mine == 0)
             def _():
-                @pl.when((i >= 1) & (i <= chunks))
-                def _():
-                    core_sum(1, yo, i - 1, False)
-                    x_sum(y, i - 1, False)
-
-                @pl.when(i >= 2)
-                def _():
-                    x_sum(yo, i - 2, False)
+                @pl.when(i < chunks)
+                def _():
+                    core_sum(1, yo, i, False)
+                    x_sum(y, i, False)
+
+                @pl.when(i >= 1)
+                def _():
+                    x_sum(yo, i - 1, False)
 
             @pl.when(mine == 1)
             def _():
-                @pl.when((i >= 1) & (i <= chunks))
+                @pl.when(i < chunks)
                 def _():
                     for slot, yr in ((0, y), (0, yo), (1, y)):
-                        core_sum(slot, yr, i - 1, True)
-
-                @pl.when(i == chunks + 1)
+                        core_sum(slot, yr, i, True)
+
+                @pl.when(i == chunks - 1)
                 def _():
                     each(chunks, lambda j: core_sum(1, yo, j, True))
 
-                @pl.when(i >= 2)
-                def _():
-                    x_sum(y, i - 2, True)
-
-                @pl.when((i >= 2) & (final == 0))
-                def _():
-                    x_sum(yo, i - 2, True)
+                @pl.when(i >= 1)
+                def _():
+                    x_sum(y, i - 1, True)
+
+                @pl.when((i >= 1) & (final == 0))
+                def _():
+                    x_sum(yo, i - 1, True)
 
         @pl.when((mine == 1) & (final == 1))
         def _():
@@ -607,10 +615,18 @@
                 def _():
                     if i == 0:
                         core_sum(1, yo, k - 2, False)
-                    if i == 1:
-                        x_sum(y, k - 2, False)
-                    if i == 3:
-                        x_sum(yo, k - 2, False)
+
+                    @pl.when(final == 1)
+                    def _():
+                        if i == 1:
+                            x_sum(y, k - 2, False)
+                        if i == 3:
+                            x_sum(yo, k - 2, False)
+
+                    @pl.when((final == 0) & (k < 4))
+                    def _():
+                        j = 2 * k - 4 + i // 2
+                        x_sum(y if i % 2 == 0 else yo, j, False)
 
     @pl.when(mine == 1)
     def _():
@@ -655,13 +671,16 @@
     return pl.pallas_call(
         functools.partial(fused_kernel, sides),
         out_shape=jax.ShapeDtypeStruct((window, 2 * rows), bf16),
-        in_specs=[hbm] * 4 + [vmem] * 3 + [hbm],
+        in_specs=[hbm] * 8,
         out_specs=vmem,
         scratch_shapes=[
             pltpu.VMEM((window, query_width), bf16),
             pltpu.VMEM((window, head_size), bf16),
             pltpu.VMEM((window, head_size), bf16),
             pltpu.VMEM((window, query_width), bf16),
+            pltpu.VMEM(lse.shape[1:], bf16),
+            pltpu.VMEM(lse.shape[1:], bf16),
+            pltpu.VMEM((1,) + segments.shape, segments.dtype),
             pltpu.VMEM((2, window, width), bf16),
             pltpu.VMEM((2, 2, rows, width), bf16),
             pltpu.VMEM((2, 2, chunks) + tile, f32),
@@ -675,7 +694,7 @@
             pltpu.VMEM(lse.shape[1:], f32),
             pltpu.VMEM((window, head_size), f32),
             pltpu.VMEM((window, head_size), f32),
-            dma((5,)),
+            dma((8,)),
             dma((pieces,)),
             dma((pieces,)),
             dma((pieces,)),
@@ -692,17 +711,22 @@
             dma((2, chunks)),
         ],
         compiler_params=pltpu.CompilerParams(
-            collective_id=0, has_side_effects=True, vmem_limit_bytes=60 * 1024 * 1024
+            collective_id=0, has_side_effects=True, vmem_limit_bytes=40 * 1024 * 1024
         ),
     )(
-        q.reshape(window, query_width),
-        k.reshape(window, head_size),
-        v.reshape(window, head_size),
-        do.reshape(window, query_width),
-        lse,
-        delta,
-        segments.reshape(1, -1),
-        weight.reshape(rows, width),
+        *(
+            pltpu.with_memory_space_constraint(array, pltpu.HBM)
+            for array in (
+                q.reshape(window, query_width),
+                k.reshape(window, head_size),
+                v.reshape(window, head_size),
+                do.reshape(window, query_width),
+                lse.reshape(lse.shape[1:]),
+                delta.reshape(delta.shape[1:]),
+                segments.reshape(1, -1),
+                weight.reshape(rows, width),
+            )
+        )
     )
 
 

time: 89.7 us -> 85.9 us (0.958)
  Pallas kernels: 87.1 us -> 84.8 us
  local copies, waits for them, and re-layouts: 2.26 us -> 0.97 us
    pallas_call x1, Pallas kernels: 87.1 us -> 84.8 us  [fused(): pl.pallas_call(functools.partial(fused_kernel, sides), out_shape=jax.Shap...]
    unnamed x1, local copies, waits for them, and re-layouts: 2.26 us -> 0.97 us
where the time goes in v3:
time: 85.9 us; the launch traced here: 85.8 us
  Pallas kernels  84.8 us (99%)
  local copies, waits for them, and re-layouts  0.97 us (1%)
    pallas_call x1, Pallas kernels, fused(): pl.pallas_call(functools.partial(fused_kernel, sides), out_shape=jax.Shap...  84.8 us

profile of v3, /device:TPU:17, one launch (start us, length us, event | category | flops | bytes accessed | tf_op | source)
XLA Modules:
  0.0 85.8 jit_solution(14143357275371505601)
XLA Ops:
  0.0 84.8 %shard_map.82 = bf16[512,1024]{1,0:T(8,128)(2,1)S(1)} custom-call(bf16[512,1024]{1,0:T(8,128)(2,1)} %bitcast.9, bf16[512,128]{1,0:T(8,128)(2,1)} %bitcast.11, bf16[512,128]{1,0:T(8,128)(2,1)} %bitcast.12, bf16[512,1024]{1,0:T(8,128)(2,1)} %bitcast.10, bf16[8,512]{1,0:T(8,128)(2,1)} %bitcast.14, bf16[8,512]{1,0:T(8,128)(2,1)} %bitcast.15, ...), custom_call_target="tpu_custom_call" | custom-call | tf_op jit(solution)/shard_map/pallas_call | solution.py:671
  84.8 1.0 %copy.10 = bf16[512,1024]{1,0:T(8,128)(2,1)} copy(bf16[512,1024]{1,0:T(8,128)(2,1)S(1)} %shard_map.82) | data formatting | bytes 2097152

commit v4 on v3

--- a/solution.py
+++ b/solution.py
@@ -171,6 +171,12 @@
     x_recv,
     back_send,
     back_recv,
+    small_part_send,
+    small_part_recv,
+    small_x_send,
+    small_x_recv,
+    small_back_send,
+    small_back_recv,
 ):
     window, head_size = k_ref.shape
     groups = q_ref.shape[1] // head_size
@@ -301,7 +307,7 @@
     def each(count, body):
         lax.fori_loop(0, count, lambda i, carry: (body(i), carry)[1], 0)
 
-    first = 2
+    first = LANES // PIECE // 4
 
     each(pieces, lambda p: own_copy(p).start())
 
@@ -426,6 +432,77 @@
                 part_out[slot, yr, k, block_rows(i)] = low[:, k * LANES : (k + 1) * LANES]
             part_copy(slot, yr, i, True).start()
 
+    def small(ref, lead, a, b):
+        return ref.at[(*lead, b, block_rows(a))]
+
+    def small_part(a, b):
+        return remote(
+            small(part_out, (1, yo), a, b),
+            small(part_in, (1, yo), a, b),
+            small_part_send.at[a, b],
+            small_part_recv.at[a, b],
+            core_peer,
+        )
+
+    def small_x(a, b):
+        return remote(
+            small(x_out, (yo,), a, b),
+            small(x_in, (yo,), a, b),
+            small_x_send.at[a, b],
+            small_x_recv.at[a, b],
+            x_peer,
+        )
+
+    def small_back(a, b):
+        return remote(
+            back_out.at[block_rows(a), out_cols(yo, b)],
+            out_ref.at[block_rows(a), out_cols(yo, b)],
+            small_back_send.at[a, b],
+            small_back_recv.at[a, b],
+            back_peer,
+        )
+
+    def small_unit(a, b):
+        value = dot(joined[1, block_rows(a)], w_all[1, yo, chunk_rows(b)], 1, 1)
+
+        @pl.when(mine == 1)
+        def _():
+            keep[1, yo, b, block_rows(a)] = value
+
+        @pl.when(mine == 0)
+        def _():
+            part_out[1, yo, b, block_rows(a)] = value.astype(jnp.bfloat16)
+            small_part(a, b).start()
+
+    def small_core_sum(a, b):
+        small_part(a, b).wait_recv()
+        kept = small(keep, (1, yo), a, b)
+        value = kept[...] + small(part_in, (1, yo), a, b)[...].astype(jnp.float32)
+
+        @pl.when(final == 1)
+        def _():
+            kept[...] = value
+
+        @pl.when(final == 0)
+        def _():
+            small(x_out, (yo,), a, b)[...] = value.astype(jnp.bfloat16)
+            small_x(a, b).start()
+
+    def small_x_sum(a, b):
+        small_x(a, b).wait_recv()
+        value = small(keep, (1, yo), a, b)[...] + small(x_in, (yo,), a, b)[...].astype(jnp.float32)
+        back_out[block_rows(a), out_cols(yo, b)] = value.astype(jnp.bfloat16)
+        small_back(a, b).start()
+
+    def added(step, body):
+        def one(j):
+            body(jnp.minimum(j, step), jnp.where(j <= step, step, j - step - 1))
+
+        each(2 * step + 1, one)
+
+    def all_small(body):
+        each(chunks * chunks, lambda j: body(j // chunks, j % chunks))
+
     def core_sum(slot, yr, i, by_token):
         part_copy(slot, yr, i, by_token).wait_recv()
         kept = tile(keep, (slot, yr), i, by_token)
@@ -474,7 +551,7 @@
     def which(i):
         return jnp.where(i // chunks % 2 == 0, y, yo)
 
-    lag = 2
+    lag, turns = 2, 4
 
     @pl.when(outer)
     def _():
@@ -516,10 +593,7 @@
                 block_unit(0, y, i)
                 block_unit(0, yo, i)
                 block_unit(1, y, i)
-
-            @pl.when(i == chunks - 1)
-            def _():
-                each(chunks, lambda j: block_unit(1, yo, j))
+                added(i, small_unit)
 
             @pl.when(mine == 0)
             def _():
@@ -538,10 +612,7 @@
                 def _():
                     for slot, yr in ((0, y), (0, yo), (1, y)):
                         core_sum(slot, yr, i, True)
-
-                @pl.when(i == chunks - 1)
-                def _():
-                    each(chunks, lambda j: core_sum(1, yo, j, True))
+                    added(i, small_core_sum)
 
                 @pl.when(i >= 1)
                 def _():
@@ -551,9 +622,9 @@
                 def _():
                     x_sum(yo, i - 1, True)
 
-        @pl.when((mine == 1) & (final == 1))
-        def _():
-            each(chunks, lambda j: x_sum(yo, j, True))
+                @pl.when((i >= 1) & (final == 1))
+                def _():
+                    added(i - 1, small_x_sum)
 
     @pl.when(jnp.logical_not(outer))
     def _():
@@ -561,13 +632,16 @@
         def _(i):
             k = i % chunks
 
-            @pl.when(i == 2 * chunks - 1)
-            def _():
-                each(chunks, lambda j: j_block(j).start())
-
             @pl.when((i >= chunks) & (i < 2 * chunks))
             def _():
-                wait_chunk(arrived_own, k)
+                for j in range(per):
+                    if j == per * 3 // 4:
+
+                        @pl.when(i == 2 * chunks - 1)
+                        def _():
+                            each(chunks, lambda b: j_block(b).start())
+
+                    arrived_own(k * per + j)
 
             @pl.when(i < 2 * chunks)
             def _():
@@ -581,21 +655,23 @@
 
         @pl.loop(0, chunks + 2)
         def _(k):
-            for i in range(per):
+            for i in range(turns):
 
                 @pl.when(k < chunks)
                 def _():
-                    arrived_far(k * per + i)
-                    relay_copy(k * per + i).start()
+                    for j in range(per // turns):
+                        p = k * per + i * (per // turns) + j
+                        arrived_far(p)
+                        relay_copy(p).start()
 
                 @pl.when(k == 0)
                 def _():
-                    for j in range(i * 2 * chunks // per, (i + 1) * 2 * chunks // per):
+                    for j in range(i * 2 * chunks // turns, (i + 1) * 2 * chunks // turns):
                         unit(0, which(j), j % chunks, 1)
 
                 @pl.when((k == 1) & (mine == 1))
                 def _():
-                    for j in range(i * 2 * chunks // per, (i + 1) * 2 * chunks // per):
+                    for j in range(i * 2 * chunks // turns, (i + 1) * 2 * chunks // turns):
                         core_sum(0, which(j), j % chunks, False)
 
                 @pl.when((k >= 1) & (k <= chunks))
@@ -623,17 +699,50 @@
                         if i == 3:
                             x_sum(yo, k - 2, False)
 
-                    @pl.when((final == 0) & (k < 4))
+                    @pl.when((final == 0) & (k < chunks))
                     def _():
-                        j = 2 * k - 4 + i // 2
-                        x_sum(y if i % 2 == 0 else yo, j, False)
-
-    @pl.when(mine == 1)
-    def _():
-        @pl.loop(0, 2 * chunks)
-        def _(i):
-            back_copy(i // chunks, i % chunks, False).wait_recv()
-            back_copy(i // chunks, i % chunks, False).wait_send()
+                        if i < 2:
+                            x_sum((y, yo)[i], 2 * k - 4, False)
+                            x_sum((y, yo)[i], 2 * k - 3, False)
+
+    inner = jnp.logical_not(outer)
+
+    def tiles(condition, copies, wait):
+        @pl.when(condition)
+        def _():
+            each(chunks, lambda i: wait(copies(i)))
+
+    def smalls(condition, copies, wait):
+        @pl.when(condition)
+        def _():
+            all_small(lambda a, b: wait(copies(a, b)))
+
+    def received(copy):
+        copy.wait_recv()
+
+    def sent(copy):
+        copy.wait_send()
+
+    back = mine == 1
+    tiles(back, lambda i: back_copy(y, i, False), received)
+    tiles(back & (outer | (final == 0)), lambda i: back_copy(yo, i, False), received)
+    smalls(back & inner & (final == 1), small_back, received)
+    tiles(back, lambda i: back_copy(y, i, False), sent)
+    tiles(back & (inner | (final == 0)), lambda i: back_copy(yo, i, False), sent)
+    smalls(back & outer & (final == 1), small_back, sent)
+    by_small = outer & (final == 0) & (mine == 1)
+    tiles(jnp.logical_not(by_small), lambda i: x_copy(yo, i, False), sent)
+    smalls(by_small, small_x, sent)
+    by_small = outer & (mine == 0)
+    tiles(jnp.logical_not(by_small), lambda i: part_copy(1, yo, i, False), sent)
+    smalls(by_small, small_part, sent)
+
+    @pl.loop(0, chunks)
+    def _(i):
+        x_copy(y, i, False).wait_send()
+        part_copy(0, y, i, False).wait_send()
+        part_copy(0, yo, i, False).wait_send()
+        part_copy(1, y, i, False).wait_send()
 
     @pl.loop(0, pieces)
     def _(p):
@@ -648,13 +757,6 @@
     @pl.when(jnp.logical_not(outer))
     def _():
         each(chunks, lambda i: j_block(i).wait_send())
-
-    @pl.loop(0, 2 * chunks)
-    def _(i):
-        yr, k = i // chunks, i % chunks
-        part_copy(0, yr, k, False).wait_send()
-        part_copy(1, yr, k, False).wait_send()
-        x_copy(yr, k, False).wait_send()
 
 
 def fused(sides, q, k, v, do, lse, delta, segments, weight):
@@ -709,6 +811,7 @@
             dma((2, chunks)),
             dma((2, chunks)),
             dma((2, chunks)),
+            *[dma((chunks, chunks))] * 6,
         ],
         compiler_params=pltpu.CompilerParams(
             collective_id=0, has_side_effects=True, vmem_limit_bytes=40 * 1024 * 1024

time: 85.9 us -> 81.4 us (0.948)
  Pallas kernels: 84.8 us -> 80.1 us
    pallas_call x1, Pallas kernels: 84.8 us -> 80.1 us  [fused(): pl.pallas_call(functools.partial(fused_kernel, sides), out_shape=jax.Shap...]
where the time goes in v4:
time: 81.4 us; the launch traced here: 81.1 us
  Pallas kernels  80.1 us (98%)
  local copies, waits for them, and re-layouts  0.97 us (1%)
    pallas_call x1, Pallas kernels, fused(): pl.pallas_call(functools.partial(fused_kernel, sides), out_shape=jax.Shap...  80.1 us

profile of v4, /device:TPU:17, one launch (start us, length us, event | category | flops | bytes accessed | tf_op | source)
XLA Modules:
  0.0 81.1 jit_solution(6568987541683925215)
XLA Ops:
  0.0 80.1 %shard_map.82 = bf16[512,1024]{1,0:T(8,128)(2,1)S(1)} custom-call(bf16[512,1024]{1,0:T(8,128)(2,1)} %bitcast.9, bf16[512,128]{1,0:T(8,128)(2,1)} %bitcast.11, bf16[512,128]{1,0:T(8,128)(2,1)} %bitcast.12, bf16[512,1024]{1,0:T(8,128)(2,1)} %bitcast.10, bf16[8,512]{1,0:T(8,128)(2,1)} %bitcast.14, bf16[8,512]{1,0:T(8,128)(2,1)} %bitcast.15, ...), custom_call_target="tpu_custom_call" | custom-call | tf_op jit(solution)/shard_map/pallas_call | solution.py:773
  80.1 1.0 %copy.10 = bf16[512,1024]{1,0:T(8,128)(2,1)} copy(bf16[512,1024]{1,0:T(8,128)(2,1)S(1)} %shard_map.82) | data formatting | bytes 2097152

commit v5 on v4

--- a/solution.py
+++ b/solution.py
@@ -192,7 +192,7 @@
     odd, upper = z % sides, z // sides
     partner = z + 1 - 2 * odd
     far = z + sides - 2 * sides * upper
-    outer = upper == odd
+    outer = upper != odd
     mine = jnp.where(c == odd, 0, 1)
     final = jnp.where(x == upper, 0, 1)
 
@@ -215,110 +215,20 @@
                 (delta_hbm, delta_ref),
                 (k_hbm, k_ref),
                 (v_hbm, v_ref),
-                (q_hbm, q_ref),
-                (do_hbm, do_ref),
+                (q_hbm.at[:, :head_size], q_ref.at[:, :head_size]),
+                (do_hbm.at[:, :head_size], do_ref.at[:, :head_size]),
+                (q_hbm.at[:, head_size:], q_ref.at[:, head_size:]),
+                (do_hbm.at[:, head_size:], do_ref.at[:, head_size:]),
                 (w_hbm, w_all.at[0, y]),
             )
         )
     ]
-    for load in loads:
-        load.start()
-
     barrier = pltpu.get_barrier_semaphore()
     peers = (y_peer, far_peer, j_peer, core_peer, x_peer, back_peer)
     for peer in peers:
         pl.semaphore_signal(barrier, inc=1, device_id=peer, device_id_type=MESH)
-    pl.semaphore_wait(barrier, len(peers))
-
-    def remote(src, dst, send, recv, peer):
-        return pltpu.make_async_remote_copy(
-            src_ref=src,
-            dst_ref=dst,
-            send_sem=send,
-            recv_sem=recv,
-            device_id=peer,
-            device_id_type=MESH,
-        )
-
-    def piece_rows(p):
-        return pl.ds(pl.multiple_of(p * PIECE, PIECE), PIECE)
-
-    def chunk_rows(k):
-        return pl.ds(pl.multiple_of(k * LANES, LANES), LANES)
-
-    def block_rows(i):
-        return pl.ds(pl.multiple_of(i * block, block), block)
-
-    def own_copy(p):
-        return remote(
-            w_hbm.at[piece_rows(p)],
-            w_all.at[0, y, piece_rows(p)],
-            own_send.at[p],
-            own_recv.at[p],
-            y_peer,
-        )
-
-    def far_copy(p):
-        return remote(
-            w_hbm.at[piece_rows(p)],
-            w_all.at[1, y, piece_rows(p)],
-            far_send.at[p],
-            far_recv.at[p],
-            far_peer,
-        )
-
-    def relay_copy(p):
-        ref = w_all.at[1, y, piece_rows(p)]
-        return remote(ref, ref, relay_send.at[p], relay_recv.at[p], y_peer)
-
-    def arrived_own(p):
-        ref = w_all.at[0, yo, piece_rows(p)]
-        remote(ref, ref, own_send.at[p], own_recv.at[p], y_peer).wait_recv()
-
-    def arrived_far(p):
-        ref = w_all.at[1, y, piece_rows(p)]
-        remote(ref, ref, far_send.at[p], far_recv.at[p], far_peer).wait_recv()
-
-    def arrived_relay(p):
-        ref = w_all.at[1, yo, piece_rows(p)]
-        remote(ref, ref, relay_send.at[p], relay_recv.at[p], y_peer).wait_recv()
-
-    def j_cols(r):
-        return pl.ds(pl.multiple_of(r * head_size, head_size), head_size)
-
-    def j_copy(r):
-        return remote(
-            joined.at[0, :, j_cols(r)],
-            joined.at[1, :, j_cols(r)],
-            j_send.at[r],
-            j_recv.at[r],
-            j_peer,
-        )
-
-    def j_block(i):
-        return remote(
-            joined.at[0, block_rows(i)],
-            joined.at[1, block_rows(i)],
-            j_send.at[i],
-            j_recv.at[i],
-            j_peer,
-        )
-
-    def each(count, body):
-        lax.fori_loop(0, count, lambda i, carry: (body(i), carry)[1], 0)
-
-    first = LANES // PIECE // 4
-
-    each(pieces, lambda p: own_copy(p).start())
-
-    @pl.when(outer)
-    def _():
-        each(first, lambda p: far_copy(p).start())
-
-    @pl.when(jnp.logical_not(outer))
-    def _():
-        each(pieces, lambda p: far_copy(p).start())
-
+    for load in loads:
+        load.start()
     for load in loads[:3]:
         load.wait()
     lse32[...] = lse_ref[...].astype(jnp.float32)
@@ -328,19 +238,16 @@
     key_id = lax.broadcasted_iota(jnp.int32, (window, window), 0)
     query_id = lax.broadcasted_iota(jnp.int32, (window, window), 1)
     bias[...] = jnp.where((seg_col == seg_row) & (key_id <= query_id), 0.0, -1e30)
-    dk_acc[...] = jnp.zeros_like(dk_acc)
-    dv_acc[...] = jnp.zeros_like(dv_acc)
+    def j_cols(r):
+        return pl.ds(pl.multiple_of(r * head_size, head_size), head_size)
+
     scale = head_size ** (-0.5)
     half = window // 2
 
     def dot(a, b, da, db):
         return lax.dot_general(a, b, (((da,), (db,)), ((), ())), preferred_element_type=jnp.float32)
 
-    for load in loads[3:7]:
-        load.wait()
-
-    @pl.loop(0, groups)
-    def _(r):
+    def head(r):
         cols = j_cols(r)
         sums = []
         for start in (0, half):
@@ -358,6 +265,111 @@
         joined[0, :half, cols] = (low[:half] * scale).astype(jnp.bfloat16)
         joined[0, half:, cols] = ((low[half:] + sums[1]) * scale).astype(jnp.bfloat16)
 
+    dk_acc[...] = jnp.zeros_like(dk_acc)
+    dv_acc[...] = jnp.zeros_like(dv_acc)
+    for load in loads[3:7]:
+        load.wait()
+
+    @pl.when(outer)
+    def _():
+        head(0)
+
+    pl.semaphore_wait(barrier, len(peers))
+
+    def remote(src, dst, send, recv, peer):
+        return pltpu.make_async_remote_copy(
+            src_ref=src,
+            dst_ref=dst,
+            send_sem=send,
+            recv_sem=recv,
+            device_id=peer,
+            device_id_type=MESH,
+        )
+
+    def piece_rows(p):
+        return pl.ds(pl.multiple_of(p * PIECE, PIECE), PIECE)
+
+    def chunk_rows(k):
+        return pl.ds(pl.multiple_of(k * LANES, LANES), LANES)
+
+    def block_rows(i):
+        return pl.ds(pl.multiple_of(i * block, block), block)
+
+    def own_copy(k):
+        return remote(
+            w_hbm.at[chunk_rows(k)],
+            w_all.at[0, y, chunk_rows(k)],
+            own_send.at[k],
+            own_recv.at[k],
+            y_peer,
+        )
+
+    def arrived_own(k):
+        ref = w_all.at[0, yo, chunk_rows(k)]
+        remote(ref, ref, own_send.at[k], own_recv.at[k], y_peer).wait_recv()
+
+    def far_copy(p, part):
+        return remote(
+            w_hbm.at[part(p)],
+            w_all.at[1, y, part(p)],
+            far_send.at[p],
+            far_recv.at[p],
+            far_peer,
+        )
+
+    def relay_copy(p, part):
+        ref = w_all.at[1, y, part(p)]
+        return remote(ref, ref, relay_send.at[p], relay_recv.at[p], y_peer)
+
+    def arrived_far(p, part):
+        ref = w_all.at[1, y, part(p)]
+        remote(ref, ref, far_send.at[p], far_recv.at[p], far_peer).wait_recv()
+
+    def arrived_relay(p, part):
+        ref = w_all.at[1, yo, part(p)]
+        remote(ref, ref, relay_send.at[p], relay_recv.at[p], y_peer).wait_recv()
+
+    def j_copy(r):
+        return remote(
+            joined.at[0, :, j_cols(r)],
+            joined.at[1, :, j_cols(r)],
+            j_send.at[r],
+            j_recv.at[r],
+            j_peer,
+        )
+
+    def j_block(i):
+        return remote(
+            joined.at[0, block_rows(i)],
+            joined.at[1, block_rows(i)],
+            j_send.at[i],
+            j_recv.at[i],
+            j_peer,
+        )
+
+    def each(count, body):
+        lax.fori_loop(0, count, lambda i, carry: (body(i), carry)[1], 0)
+
+    @pl.when(outer)
+    def _():
+        j_copy(0).start()
+        each(chunks, lambda k: own_copy(k).start())
+
+    @pl.when(jnp.logical_not(outer))
+    def _():
+        def both(k):
+            far_copy(k, chunk_rows).start()
+            own_copy(k).start()
+
+        each(chunks, both)
+
+    for load in loads[7:9]:
+        load.wait()
+
+    @pl.loop(jnp.where(outer, 1, 0), groups)
+    def _(r):
+        head(r)
+
         @pl.when(outer)
         def _():
             j_copy(r).start()
@@ -365,7 +377,7 @@
     wide = groups * head_size
     joined[0, :, wide : wide + head_size] = (dk_acc[...] * scale).astype(jnp.bfloat16)
     joined[0, :, wide + head_size : wide + 2 * head_size] = dv_acc[...].astype(jnp.bfloat16)
-    loads[7].wait()
+    loads[9].wait()
 
     def tile(ref, lead, i, by_token):
         return ref.at[(*lead, slice(None), block_rows(i))] if by_token else ref.at[(*lead, i)]
@@ -544,10 +556,6 @@
                 put(back_out)
                 back_copy(yr, i, False).start()
 
-    def wait_chunk(arrived, k):
-        for i in range(per):
-            arrived(k * per + i)
-
     def which(i):
         return jnp.where(i // chunks % 2 == 0, y, yo)
 
@@ -557,23 +565,18 @@
     def _():
         j_copy(groups).start()
         j_copy(groups + 1).start()
-        each(pieces - first, lambda p: far_copy(p + first).start())
+        each(pieces, lambda p: far_copy(p, piece_rows).start())
         steps = 3 * chunks
-        share = pieces // (2 * chunks)
 
         @pl.loop(0, steps + lag)
         def _(i):
             k = i % chunks
 
-            @pl.when(i < 2 * chunks)
-            def _():
-                for j in range(share):
-                    arrived_far(i * share + j)
-                    relay_copy(i * share + j).start()
-
             @pl.when((i >= chunks) & (i < 2 * chunks))
             def _():
-                wait_chunk(arrived_own, k)
+                arrived_far(k, chunk_rows)
+                relay_copy(k, chunk_rows).start()
+                arrived_own(k)
 
             @pl.when(i < steps)
             def _():
@@ -585,63 +588,83 @@
 
         @pl.loop(0, chunks + 1)
         def _(i):
-            @pl.when(i < chunks)
-            def _():
-                wait_chunk(arrived_relay, i)
+            live = i < chunks
+
+            def partner_sum(slot, yr):
+                @pl.when(live & (mine == 1))
+                def _():
+                    core_sum(slot, yr, i, True)
+
+            @pl.when(live)
+            def _():
+                arrived_relay(i, chunk_rows)
+
+            @pl.when(live)
+            def _():
                 unit(1, yo, i, 0)
+
+            @pl.when(live)
+            def _():
                 j_block(i).wait_recv()
+
+            @pl.when(live)
+            def _():
+                block_unit(1, y, i)
+
+            @pl.when(live)
+            def _():
                 block_unit(0, y, i)
+
+            partner_sum(1, y)
+            @pl.when(live)
+            def _():
                 block_unit(0, yo, i)
-                block_unit(1, y, i)
+
+            partner_sum(0, y)
+            @pl.when(live)
+            def _():
                 added(i, small_unit)
 
+            partner_sum(0, yo)
+            @pl.when((i >= 1) & (mine == 1))
+            def _():
+                x_sum(y, i - 1, True)
+
+                @pl.when(final == 0)
+                def _():
+                    x_sum(yo, i - 1, True)
+
+                @pl.when(final == 1)
+                def _():
+                    added(i - 1, small_x_sum)
+
+            @pl.when(live & (mine == 1))
+            def _():
+                added(i, small_core_sum)
+
             @pl.when(mine == 0)
             def _():
-                @pl.when(i < chunks)
+                @pl.when(i >= 1)
+                def _():
+                    x_sum(yo, i - 1, False)
+
+                @pl.when(live)
                 def _():
                     core_sum(1, yo, i, False)
                     x_sum(y, i, False)
 
-                @pl.when(i >= 1)
-                def _():
-                    x_sum(yo, i - 1, False)
-
-            @pl.when(mine == 1)
-            def _():
-                @pl.when(i < chunks)
-                def _():
-                    for slot, yr in ((0, y), (0, yo), (1, y)):
-                        core_sum(slot, yr, i, True)
-                    added(i, small_core_sum)
-
-                @pl.when(i >= 1)
-                def _():
-                    x_sum(y, i - 1, True)
-
-                @pl.when((i >= 1) & (final == 0))
-                def _():
-                    x_sum(yo, i - 1, True)
-
-                @pl.when((i >= 1) & (final == 1))
-                def _():
-                    added(i - 1, small_x_sum)
-
     @pl.when(jnp.logical_not(outer))
     def _():
+        each(chunks, lambda b: j_block(b).start())
+
         @pl.loop(0, 2 * chunks + lag)
         def _(i):
             k = i % chunks
 
             @pl.when((i >= chunks) & (i < 2 * chunks))
             def _():
-                for j in range(per):
-                    if j == per * 3 // 4:
-
-                        @pl.when(i == 2 * chunks - 1)
-                        def _():
-                            each(chunks, lambda b: j_block(b).start())
-
-                    arrived_own(k * per + j)
+                arrived_own(k)
+
 
             @pl.when(i < 2 * chunks)
             def _():
@@ -661,8 +684,8 @@
                 def _():
                     for j in range(per // turns):
                         p = k * per + i * (per // turns) + j
-                        arrived_far(p)
-                        relay_copy(p).start()
+                        arrived_far(p, piece_rows)
+                        relay_copy(p, piece_rows).start()
 
                 @pl.when(k == 0)
                 def _():
@@ -678,25 +701,27 @@
                 def _():
                     if i == 0:
                         unit(1, y, k - 1, 0)
+                        unit(1, y, k - 1, 1)
                     if i == 1:
-                        unit(1, y, k - 1, 1)
+                        core_sum(1, y, k - 1, False)
                     if i == 2:
-                        wait_chunk(arrived_relay, k - 1)
+                        for j in range(per):
+                            arrived_relay((k - 1) * per + j, piece_rows)
                         unit(1, yo, k - 1, 0)
-                        core_sum(1, y, k - 1, False)
+                        unit(1, yo, k - 1, 1)
                     if i == 3:
-                        unit(1, yo, k - 1, 1)
+                        core_sum(1, yo, k - 1, False)
+
+                        @pl.when(final == 1)
+                        def _():
+                            x_sum(y, k - 1, False)
 
                 @pl.when(k >= 2)
                 def _():
                     if i == 0:
-                        core_sum(1, yo, k - 2, False)
-
-                    @pl.when(final == 1)
-                    def _():
-                        if i == 1:
-                            x_sum(y, k - 2, False)
-                        if i == 3:
+
+                        @pl.when(final == 1)
+                        def _():
                             x_sum(yo, k - 2, False)
 
                     @pl.when((final == 0) & (k < chunks))
@@ -744,11 +769,17 @@
         part_copy(0, yo, i, False).wait_send()
         part_copy(1, y, i, False).wait_send()
 
-    @pl.loop(0, pieces)
-    def _(p):
-        own_copy(p).wait_send()
-        far_copy(p).wait_send()
-        relay_copy(p).wait_send()
+    each(chunks, lambda k: own_copy(k).wait_send())
+
+    @pl.when(outer)
+    def _():
+        each(pieces, lambda p: far_copy(p, piece_rows).wait_send())
+        each(chunks, lambda k: relay_copy(k, chunk_rows).wait_send())
+
+    @pl.when(inner)
+    def _():
+        each(chunks, lambda k: far_copy(k, chunk_rows).wait_send())
+        each(pieces, lambda p: relay_copy(p, piece_rows).wait_send())
 
     @pl.when(outer)
     def _():
@@ -796,7 +827,7 @@
             pltpu.VMEM(lse.shape[1:], f32),
             pltpu.VMEM((window, head_size), f32),
             pltpu.VMEM((window, head_size), f32),
-            dma((8,)),
+            dma((10,)),
             dma((pieces,)),
             dma((pieces,)),
             dma((pieces,)),

time: 81.4 us -> 80.1 us (0.984)
  Pallas kernels: 80.1 us -> 78.9 us
    pallas_call x1, Pallas kernels: 80.1 us -> 78.9 us  [fused(): pl.pallas_call(functools.partial(fused_kernel, sides), out_shape=jax.Shap...]
where the time goes in v5:
time: 80.1 us; the launch traced here: 79.8 us
  Pallas kernels  78.9 us (99%)
  local copies, waits for them, and re-layouts  0.97 us (1%)
    pallas_call x1, Pallas kernels, fused(): pl.pallas_call(functools.partial(fused_kernel, sides), out_shape=jax.Shap...  78.9 us

profile of v5, /device:TPU:17, one launch (start us, length us, event | category | flops | bytes accessed | tf_op | source)
XLA Modules:
  0.0 79.8 jit_solution(8555812303138797348)
XLA Ops:
  0.0 78.9 %shard_map.82 = bf16[512,1024]{1,0:T(8,128)(2,1)S(1)} custom-call(bf16[512,1024]{1,0:T(8,128)(2,1)} %bitcast.9, bf16[512,128]{1,0:T(8,128)(2,1)} %bitcast.11, bf16[512,128]{1,0:T(8,128)(2,1)} %bitcast.12, bf16[512,1024]{1,0:T(8,128)(2,1)} %bitcast.10, bf16[8,512]{1,0:T(8,128)(2,1)} %bitcast.14, bf16[8,512]{1,0:T(8,128)(2,1)} %bitcast.15, ...), custom_call_target="tpu_custom_call" | custom-call | tf_op jit(solution)/shard_map/pallas_call | solution.py:804
  78.9 1.0 %copy.10 = bf16[512,1024]{1,0:T(8,128)(2,1)} copy(bf16[512,1024]{1,0:T(8,128)(2,1)S(1)} %shard_map.82) | data formatting | bytes 2097152

commit v6 on v5

--- a/solution.py
+++ b/solution.py
@@ -151,6 +151,8 @@
     x_out,
     x_in,
     back_out,
+    direct_out,
+    direct_in,
     bias,
     lse32,
     delta32,
@@ -177,6 +179,8 @@
     small_x_recv,
     small_back_send,
     small_back_recv,
+    direct_send,
+    direct_recv,
 ):
     window, head_size = k_ref.shape
     groups = q_ref.shape[1] // head_size
@@ -192,7 +196,8 @@
     odd, upper = z % sides, z // sides
     partner = z + 1 - 2 * odd
     far = z + sides - 2 * sides * upper
-    outer = upper != odd
+    middle = upper != odd
+    ends = jnp.logical_not(middle)
     mine = jnp.where(c == odd, 0, 1)
     final = jnp.where(x == upper, 0, 1)
 
@@ -224,20 +229,13 @@
         )
     ]
     barrier = pltpu.get_barrier_semaphore()
-    peers = (y_peer, far_peer, j_peer, core_peer, x_peer, back_peer)
+    cross_peer = device(partner, y, xo, co)
+    peers = (y_peer, far_peer, j_peer, core_peer, x_peer, back_peer, cross_peer)
     for peer in peers:
         pl.semaphore_signal(barrier, inc=1, device_id=peer, device_id_type=MESH)
     for load in loads:
         load.start()
-    for load in loads[:3]:
-        load.wait()
-    lse32[...] = lse_ref[...].astype(jnp.float32)
-    delta32[...] = delta_ref[...].astype(jnp.float32)
-    seg_row = seg_ref[:, pl.ds(pl.multiple_of(tok * window, LANES), window)].astype(jnp.float32)
-    seg_col = jnp.transpose(jnp.broadcast_to(seg_row, (LANES, window)))[:, :1]
-    key_id = lax.broadcasted_iota(jnp.int32, (window, window), 0)
-    query_id = lax.broadcasted_iota(jnp.int32, (window, window), 1)
-    bias[...] = jnp.where((seg_col == seg_row) & (key_id <= query_id), 0.0, -1e30)
+
     def j_cols(r):
         return pl.ds(pl.multiple_of(r * head_size, head_size), head_size)
 
@@ -265,17 +263,6 @@
         joined[0, :half, cols] = (low[:half] * scale).astype(jnp.bfloat16)
         joined[0, half:, cols] = ((low[half:] + sums[1]) * scale).astype(jnp.bfloat16)
 
-    dk_acc[...] = jnp.zeros_like(dk_acc)
-    dv_acc[...] = jnp.zeros_like(dv_acc)
-    for load in loads[3:7]:
-        load.wait()
-
-    @pl.when(outer)
-    def _():
-        head(0)
-
-    pl.semaphore_wait(barrier, len(peers))
-
     def remote(src, dst, send, recv, peer):
         return pltpu.make_async_remote_copy(
             src_ref=src,
@@ -350,27 +337,48 @@
     def each(count, body):
         lax.fori_loop(0, count, lambda i, carry: (body(i), carry)[1], 0)
 
-    @pl.when(outer)
+    def enter():
+        pl.semaphore_wait(barrier, len(peers))
+
+    @pl.when(ends)
     def _():
-        j_copy(0).start()
-        each(chunks, lambda k: own_copy(k).start())
-
-    @pl.when(jnp.logical_not(outer))
-    def _():
+        enter()
+
         def both(k):
             far_copy(k, chunk_rows).start()
             own_copy(k).start()
 
         each(chunks, both)
 
+    for load in loads[:3]:
+        load.wait()
+    lse32[...] = lse_ref[...].astype(jnp.float32)
+    delta32[...] = delta_ref[...].astype(jnp.float32)
+    seg_row = seg_ref[:, pl.ds(pl.multiple_of(tok * window, LANES), window)].astype(jnp.float32)
+    seg_col = jnp.transpose(jnp.broadcast_to(seg_row, (LANES, window)))[:, :1]
+    key_id = lax.broadcasted_iota(jnp.int32, (window, window), 0)
+    query_id = lax.broadcasted_iota(jnp.int32, (window, window), 1)
+    bias[...] = jnp.where((seg_col == seg_row) & (key_id <= query_id), 0.0, -1e30)
+    dk_acc[...] = jnp.zeros_like(dk_acc)
+    dv_acc[...] = jnp.zeros_like(dv_acc)
+    for load in loads[3:7]:
+        load.wait()
+
+    @pl.when(middle)
+    def _():
+        head(0)
+        enter()
+        j_copy(0).start()
+        each(chunks, lambda k: own_copy(k).start())
+
     for load in loads[7:9]:
         load.wait()
 
-    @pl.loop(jnp.where(outer, 1, 0), groups)
+    @pl.loop(jnp.where(middle, 1, 0), groups)
     def _(r):
         head(r)
 
-        @pl.when(outer)
+        @pl.when(middle)
         def _():
             j_copy(r).start()
 
@@ -505,6 +513,46 @@
         value = small(keep, (1, yo), a, b)[...] + small(x_in, (yo,), a, b)[...].astype(jnp.float32)
         back_out[block_rows(a), out_cols(yo, b)] = value.astype(jnp.bfloat16)
         small_back(a, b).start()
+
+    end = chunks - 1
+
+    def direct_copy(yr, source, peer):
+        return remote(
+            direct_out.at[yr],
+            direct_in.at[source, yr],
+            direct_send.at[yr],
+            direct_recv.at[source, yr],
+            peer,
+        )
+
+    def direct_sum(yr):
+        part_copy(1, yr, end, False).wait_recv()
+        value = keep[1, yr, end] + part_in[1, yr, end].astype(jnp.float32)
+        direct_out[yr] = value.astype(jnp.bfloat16)
+
+        @pl.when(final == 1)
+        def _():
+            direct_copy(yr, 0, back_peer).start()
+
+        @pl.when(final == 0)
+        def _():
+            direct_copy(yr, 1, cross_peer).start()
+
+    def far_sum(yr, k):
+        whole = (k == end) & (mine == 1)
+
+        @pl.when(whole)
+        def _():
+            direct_sum(yr)
+
+        @pl.when(jnp.logical_not(whole))
+        def _():
+            core_sum(1, yr, k, False)
+
+    def far_x_sum(yr, k):
+        @pl.when((final == 1) & ((k < end) | (mine == 0)))
+        def _():
+            x_sum(yr, k, False)
 
     def added(step, body):
         def one(j):
@@ -561,7 +609,7 @@
 
     lag, turns = 2, 4
 
-    @pl.when(outer)
+    @pl.when(middle)
     def _():
         j_copy(groups).start()
         j_copy(groups + 1).start()
@@ -597,35 +645,22 @@
 
             @pl.when(live)
             def _():
-                arrived_relay(i, chunk_rows)
+                j_block(i).wait_recv()
 
             @pl.when(live)
             def _():
-                unit(1, yo, i, 0)
+                block_unit(1, y, i)
 
             @pl.when(live)
             def _():
-                j_block(i).wait_recv()
+                block_unit(0, y, i)
 
             @pl.when(live)
             def _():
-                block_unit(1, y, i)
-
-            @pl.when(live)
-            def _():
-                block_unit(0, y, i)
+                block_unit(0, yo, i)
 
             partner_sum(1, y)
-            @pl.when(live)
-            def _():
-                block_unit(0, yo, i)
-
             partner_sum(0, y)
-            @pl.when(live)
-            def _():
-                added(i, small_unit)
-
-            partner_sum(0, yo)
             @pl.when((i >= 1) & (mine == 1))
             def _():
                 x_sum(y, i - 1, True)
@@ -638,9 +673,22 @@
                 def _():
                     added(i - 1, small_x_sum)
 
+            partner_sum(0, yo)
+            @pl.when(live)
+            def _():
+                arrived_relay(i, chunk_rows)
+
+            @pl.when(live)
+            def _():
+                added(i, small_unit)
+
             @pl.when(live & (mine == 1))
             def _():
                 added(i, small_core_sum)
+
+            @pl.when(live)
+            def _():
+                unit(1, yo, i, 0)
 
             @pl.when(mine == 0)
             def _():
@@ -653,7 +701,7 @@
                     core_sum(1, yo, i, False)
                     x_sum(y, i, False)
 
-    @pl.when(jnp.logical_not(outer))
+    @pl.when(ends)
     def _():
         each(chunks, lambda b: j_block(b).start())
 
@@ -700,29 +748,23 @@
                 @pl.when((k >= 1) & (k <= chunks))
                 def _():
                     if i == 0:
+                        unit(1, y, k - 1, 1)
                         unit(1, y, k - 1, 0)
-                        unit(1, y, k - 1, 1)
                     if i == 1:
-                        core_sum(1, y, k - 1, False)
+                        far_sum(y, k - 1)
                     if i == 2:
                         for j in range(per):
                             arrived_relay((k - 1) * per + j, piece_rows)
+                        unit(1, yo, k - 1, 1)
                         unit(1, yo, k - 1, 0)
-                        unit(1, yo, k - 1, 1)
                     if i == 3:
-                        core_sum(1, yo, k - 1, False)
-
-                        @pl.when(final == 1)
-                        def _():
-                            x_sum(y, k - 1, False)
+                        far_sum(yo, k - 1)
+                        far_x_sum(y, k - 1)
 
                 @pl.when(k >= 2)
                 def _():
                     if i == 0:
-
-                        @pl.when(final == 1)
-                        def _():
-                            x_sum(yo, k - 2, False)
+                        far_x_sum(yo, k - 2)
 
                     @pl.when((final == 0) & (k < chunks))
                     def _():
@@ -730,12 +772,11 @@
                             x_sum((y, yo)[i], 2 * k - 4, False)
                             x_sum((y, yo)[i], 2 * k - 3, False)
 
-    inner = jnp.logical_not(outer)
-
-    def tiles(condition, copies, wait):
+
+    def tiles(condition, copies, wait, count=chunks):
         @pl.when(condition)
         def _():
-            each(chunks, lambda i: wait(copies(i)))
+            each(count, lambda i: wait(copies(i)))
 
     def smalls(condition, copies, wait):
         @pl.when(condition)
@@ -749,43 +790,60 @@
         copy.wait_send()
 
     back = mine == 1
-    tiles(back, lambda i: back_copy(y, i, False), received)
-    tiles(back & (outer | (final == 0)), lambda i: back_copy(yo, i, False), received)
-    smalls(back & inner & (final == 1), small_back, received)
-    tiles(back, lambda i: back_copy(y, i, False), sent)
-    tiles(back & (inner | (final == 0)), lambda i: back_copy(yo, i, False), sent)
-    smalls(back & outer & (final == 1), small_back, sent)
-    by_small = outer & (final == 0) & (mine == 1)
-    tiles(jnp.logical_not(by_small), lambda i: x_copy(yo, i, False), sent)
+    count_in = jnp.where(middle & (final == 1), end, chunks)
+    count_out = jnp.where(ends & (final == 1), end, chunks)
+    count_x = jnp.where(ends & back & (final == 0), end, chunks)
+    tiles(back, lambda i: back_copy(y, i, False), received, count_in)
+    tiles(back & (middle | (final == 0)), lambda i: back_copy(yo, i, False), received, count_in)
+    smalls(back & ends & (final == 1), small_back, received)
+
+    @pl.when(back & middle & (final == 1))
+    def _():
+        for yr in (y, yo):
+            direct_copy(yr, 0, back_peer).wait_recv()
+            direct_copy(yr, 1, back_peer).wait_recv()
+            value = direct_in[0, yr].astype(jnp.float32) + direct_in[1, yr].astype(jnp.float32)
+            out_ref[:, out_cols(yr, end)] = value.astype(jnp.bfloat16)
+
+    @pl.when(back & ends)
+    def _():
+        direct_copy(y, 0, back_peer).wait_send()
+        direct_copy(yo, 0, back_peer).wait_send()
+
+    tiles(back, lambda i: back_copy(y, i, False), sent, count_out)
+    tiles(back & (ends | (final == 0)), lambda i: back_copy(yo, i, False), sent, count_out)
+    smalls(back & middle & (final == 1), small_back, sent)
+    by_small = middle & (final == 0) & (mine == 1)
+    tiles(jnp.logical_not(by_small), lambda i: x_copy(yo, i, False), sent, count_x)
+    tiles(True, lambda i: x_copy(y, i, False), sent, count_x)
     smalls(by_small, small_x, sent)
-    by_small = outer & (mine == 0)
+    by_small = middle & (mine == 0)
     tiles(jnp.logical_not(by_small), lambda i: part_copy(1, yo, i, False), sent)
     smalls(by_small, small_part, sent)
 
     @pl.loop(0, chunks)
     def _(i):
-        x_copy(y, i, False).wait_send()
         part_copy(0, y, i, False).wait_send()
         part_copy(0, yo, i, False).wait_send()
         part_copy(1, y, i, False).wait_send()
 
     each(chunks, lambda k: own_copy(k).wait_send())
 
-    @pl.when(outer)
+    @pl.when(middle)
     def _():
         each(pieces, lambda p: far_copy(p, piece_rows).wait_send())
         each(chunks, lambda k: relay_copy(k, chunk_rows).wait_send())
 
-    @pl.when(inner)
+    @pl.when(ends)
     def _():
         each(chunks, lambda k: far_copy(k, chunk_rows).wait_send())
         each(pieces, lambda p: relay_copy(p, piece_rows).wait_send())
 
-    @pl.when(outer)
+    @pl.when(middle)
     def _():
         each(columns, lambda r: j_copy(r).wait_send())
 
-    @pl.when(jnp.logical_not(outer))
+    @pl.when(ends)
     def _():
         each(chunks, lambda i: j_block(i).wait_send())
 
@@ -822,6 +880,8 @@
             pltpu.VMEM((2, chunks) + tile, bf16),
             pltpu.VMEM((2, chunks) + tile, bf16),
             pltpu.VMEM((window, 2 * rows), bf16),
+            pltpu.VMEM((2,) + tile, bf16),
+            pltpu.VMEM((2, 2) + tile, bf16),
             pltpu.VMEM((window, window), f32),
             pltpu.VMEM(lse.shape[1:], f32),
             pltpu.VMEM(lse.shape[1:], f32),
@@ -843,6 +903,8 @@
             dma((2, chunks)),
             dma((2, chunks)),
             *[dma((chunks, chunks))] * 6,
+            dma((2,)),
+            dma((2, 2)),
         ],
         compiler_params=pltpu.CompilerParams(
             collective_id=0, has_side_effects=True, vmem_limit_bytes=40 * 1024 * 1024

time: 80.1 us -> 79.3 us (0.990)
  no operation moved by 1% of the time
where the time goes in v6:
time: 79.3 us; the launch traced here: 79.2 us
  Pallas kernels  78.2 us (99%)
  local copies, waits for them, and re-layouts  0.97 us (1%)
    pallas_call x1, Pallas kernels, fused(): pl.pallas_call(functools.partial(fused_kernel, sides), out_shape=jax.Shap...  78.2 us

profile of v6, /device:TPU:17, one launch (start us, length us, event | category | flops | bytes accessed | tf_op | source)
XLA Modules:
  0.0 79.2 jit_solution(9990457128671293039)
XLA Ops:
  0.0 78.2 %shard_map.82 = bf16[512,1024]{1,0:T(8,128)(2,1)S(1)} custom-call(bf16[512,1024]{1,0:T(8,128)(2,1)} %bitcast.9, bf16[512,128]{1,0:T(8,128)(2,1)} %bitcast.11, bf16[512,128]{1,0:T(8,128)(2,1)} %bitcast.12, bf16[512,1024]{1,0:T(8,128)(2,1)} %bitcast.10, bf16[8,512]{1,0:T(8,128)(2,1)} %bitcast.14, bf16[8,512]{1,0:T(8,128)(2,1)} %bitcast.15, ...), custom_call_target="tpu_custom_call" | custom-call | tf_op jit(solution)/shard_map/pallas_call | solution.py:862
  78.2 1.0 %copy.10 = bf16[512,1024]{1,0:T(8,128)(2,1)} copy(bf16[512,1024]{1,0:T(8,128)(2,1)S(1)} %shard_map.82) | data formatting | bytes 2097152

commit v7 on v6

--- a/solution.py
+++ b/solution.py
@@ -233,8 +233,6 @@
     peers = (y_peer, far_peer, j_peer, core_peer, x_peer, back_peer, cross_peer)
     for peer in peers:
         pl.semaphore_signal(barrier, inc=1, device_id=peer, device_id_type=MESH)
-    for load in loads:
-        load.start()
 
     def j_cols(r):
         return pl.ds(pl.multiple_of(r * head_size, head_size), head_size)
@@ -340,6 +338,14 @@
     def enter():
         pl.semaphore_wait(barrier, len(peers))
 
+    def load_all():
+        for load in loads:
+            load.start()
+
+    @pl.when(middle)
+    def _():
+        load_all()
+
     @pl.when(ends)
     def _():
         enter()
@@ -349,6 +355,7 @@
             own_copy(k).start()
 
         each(chunks, both)
+        load_all()
 
     for load in loads[:3]:
         load.wait()
@@ -516,43 +523,37 @@
 
     end = chunks - 1
 
-    def direct_copy(yr, source, peer):
-        return remote(
-            direct_out.at[yr],
-            direct_in.at[source, yr],
-            direct_send.at[yr],
-            direct_recv.at[source, yr],
-            peer,
-        )
-
-    def direct_sum(yr):
-        part_copy(1, yr, end, False).wait_recv()
-        value = keep[1, yr, end] + part_in[1, yr, end].astype(jnp.float32)
-        direct_out[yr] = value.astype(jnp.bfloat16)
+    def direct_copy(source, peer):
+        return remote(direct_out, direct_in.at[source], direct_send, direct_recv.at[source], peer)
+
+    def direct_sum():
+        part_copy(1, yo, end, False).wait_recv()
+        value = keep[1, yo, end] + part_in[1, yo, end].astype(jnp.float32)
+        direct_out[...] = value.astype(jnp.bfloat16)
 
         @pl.when(final == 1)
         def _():
-            direct_copy(yr, 0, back_peer).start()
+            direct_copy(0, back_peer).start()
 
         @pl.when(final == 0)
         def _():
-            direct_copy(yr, 1, cross_peer).start()
-
-    def far_sum(yr, k):
+            direct_copy(1, cross_peer).start()
+
+    def relayed_sum(k):
         whole = (k == end) & (mine == 1)
 
         @pl.when(whole)
         def _():
-            direct_sum(yr)
+            direct_sum()
 
         @pl.when(jnp.logical_not(whole))
         def _():
-            core_sum(1, yr, k, False)
-
-    def far_x_sum(yr, k):
+            core_sum(1, yo, k, False)
+
+    def relayed_x_sum(k):
         @pl.when((final == 1) & ((k < end) | (mine == 0)))
         def _():
-            x_sum(yr, k, False)
+            x_sum(yo, k, False)
 
     def added(step, body):
         def one(j):
@@ -751,20 +752,23 @@
                         unit(1, y, k - 1, 1)
                         unit(1, y, k - 1, 0)
                     if i == 1:
-                        far_sum(y, k - 1)
+                        core_sum(1, y, k - 1, False)
                     if i == 2:
                         for j in range(per):
                             arrived_relay((k - 1) * per + j, piece_rows)
                         unit(1, yo, k - 1, 1)
                         unit(1, yo, k - 1, 0)
                     if i == 3:
-                        far_sum(yo, k - 1)
-                        far_x_sum(y, k - 1)
+                        relayed_sum(k - 1)
+
+                        @pl.when(final == 1)
+                        def _():
+                            x_sum(y, k - 1, False)
 
                 @pl.when(k >= 2)
                 def _():
                     if i == 0:
-                        far_x_sum(yo, k - 2)
+                        relayed_x_sum(k - 2)
 
                     @pl.when((final == 0) & (k < chunks))
                     def _():
@@ -793,29 +797,27 @@
     count_in = jnp.where(middle & (final == 1), end, chunks)
     count_out = jnp.where(ends & (final == 1), end, chunks)
     count_x = jnp.where(ends & back & (final == 0), end, chunks)
-    tiles(back, lambda i: back_copy(y, i, False), received, count_in)
+    tiles(back, lambda i: back_copy(y, i, False), received)
     tiles(back & (middle | (final == 0)), lambda i: back_copy(yo, i, False), received, count_in)
     smalls(back & ends & (final == 1), small_back, received)
 
     @pl.when(back & middle & (final == 1))
     def _():
-        for yr in (y, yo):
-            direct_copy(yr, 0, back_peer).wait_recv()
-            direct_copy(yr, 1, back_peer).wait_recv()
-            value = direct_in[0, yr].astype(jnp.float32) + direct_in[1, yr].astype(jnp.float32)
-            out_ref[:, out_cols(yr, end)] = value.astype(jnp.bfloat16)
+        direct_copy(0, back_peer).wait_recv()
+        direct_copy(1, back_peer).wait_recv()
+        value = direct_in[0].astype(jnp.float32) + direct_in[1].astype(jnp.float32)
+        out_ref[:, out_cols(yo, end)] = value.astype(jnp.bfloat16)
 
     @pl.when(back & ends)
     def _():
-        direct_copy(y, 0, back_peer).wait_send()
-        direct_copy(yo, 0, back_peer).wait_send()
-
-    tiles(back, lambda i: back_copy(y, i, False), sent, count_out)
+        direct_copy(0, back_peer).wait_send()
+
+    tiles(back, lambda i: back_copy(y, i, False), sent)
     tiles(back & (ends | (final == 0)), lambda i: back_copy(yo, i, False), sent, count_out)
     smalls(back & middle & (final == 1), small_back, sent)
     by_small = middle & (final == 0) & (mine == 1)
     tiles(jnp.logical_not(by_small), lambda i: x_copy(yo, i, False), sent, count_x)
-    tiles(True, lambda i: x_copy(y, i, False), sent, count_x)
+    tiles(True, lambda i: x_copy(y, i, False), sent)
     smalls(by_small, small_x, sent)
     by_small = middle & (mine == 0)
     tiles(jnp.logical_not(by_small), lambda i: part_copy(1, yo, i, False), sent)
@@ -880,8 +882,8 @@
             pltpu.VMEM((2, chunks) + tile, bf16),
             pltpu.VMEM((2, chunks) + tile, bf16),
             pltpu.VMEM((window, 2 * rows), bf16),
+            pltpu.VMEM(tile, bf16),
             pltpu.VMEM((2,) + tile, bf16),
-            pltpu.VMEM((2, 2) + tile, bf16),
             pltpu.VMEM((window, window), f32),
             pltpu.VMEM(lse.shape[1:], f32),
             pltpu.VMEM(lse.shape[1:], f32),
@@ -903,8 +905,8 @@
             dma((2, chunks)),
             dma((2, chunks)),
             *[dma((chunks, chunks))] * 6,
+            dma,
             dma((2,)),
-            dma((2, 2)),
         ],
         compiler_params=pltpu.CompilerParams(
             collective_id=0, has_side_effects=True, vmem_limit_bytes=40 * 1024 * 1024

time: 79.3 us -> 79.1 us (level)
  no operation moved by 1% of the time
where the time goes in v7:
time: 79.1 us; the launch traced here: 78.8 us
  Pallas kernels  77.8 us (98%)
  local copies, waits for them, and re-layouts  0.97 us (1%)
    pallas_call x1, Pallas kernels, fused(): pl.pallas_call(functools.partial(fused_kernel, sides), out_shape=jax.Shap...  77.8 us

profile of v7, /device:TPU:17, one launch (start us, length us, event | category | flops | bytes accessed | tf_op | source)
XLA Modules:
  0.0 78.8 jit_solution(9236104279186981244)
XLA Ops:
  0.0 77.8 %shard_map.82 = bf16[512,1024]{1,0:T(8,128)(2,1)S(1)} custom-call(bf16[512,1024]{1,0:T(8,128)(2,1)} %bitcast.9, bf16[512,128]{1,0:T(8,128)(2,1)} %bitcast.11, bf16[512,128]{1,0:T(8,128)(2,1)} %bitcast.12, bf16[512,1024]{1,0:T(8,128)(2,1)} %bitcast.10, bf16[8,512]{1,0:T(8,128)(2,1)} %bitcast.14, bf16[8,512]{1,0:T(8,128)(2,1)} %bitcast.15, ...), custom_call_target="tpu_custom_call" | custom-call | tf_op jit(solution)/shard_map/pallas_call | solution.py:864
  77.9 1.0 %copy.10 = bf16[512,1024]{1,0:T(8,128)(2,1)} copy(bf16[512,1024]{1,0:T(8,128)(2,1)S(1)} %shard_map.82) | data formatting | bytes 2097152

commit v8 on v7

--- a/solution.py
+++ b/solution.py
@@ -946,7 +946,7 @@
         window, kv_dev, _ = args[0].shape
         rows = args[7].shape[0]
         paired = sides == 2 and heads == sides * sides and tok == heads * sides and kv_dev == 1
-        if paired and rows % LANES == 0 and window % (2 * LANES) == 0 and args[1].shape[2] == LANES:
+        if paired and rows == heads * LANES and window == rows and args[1].shape[2] == LANES:
             return fused(sides, *args)
         return on_device(*args)
 

time: 79.1 us -> 79.1 us (level)
  no operation moved by 1% of the time
where the time goes in v8:
time: 79.1 us; the launch traced here: 78.8 us
  Pallas kernels  77.8 us (98%)
  local copies, waits for them, and re-layouts  0.97 us (1%)
    pallas_call x1, Pallas kernels, fused(): pl.pallas_call(functools.partial(fused_kernel, sides), out_shape=jax.Shap...  77.8 us

profile of v8, /device:TPU:17, one launch (start us, length us, event | category | flops | bytes accessed | tf_op | source)
XLA Modules:
  0.0 78.8 jit_solution(9236104279186981244)
XLA Ops:
  0.0 77.8 %shard_map.82 = bf16[512,1024]{1,0:T(8,128)(2,1)S(1)} custom-call(bf16[512,1024]{1,0:T(8,128)(2,1)} %bitcast.9, bf16[512,128]{1,0:T(8,128)(2,1)} %bitcast.11, bf16[512,128]{1,0:T(8,128)(2,1)} %bitcast.12, bf16[512,1024]{1,0:T(8,128)(2,1)} %bitcast.10, bf16[8,512]{1,0:T(8,128)(2,1)} %bitcast.14, bf16[8,512]{1,0:T(8,128)(2,1)} %bitcast.15, ...), custom_call_target="tpu_custom_call" | custom-call | tf_op jit(solution)/shard_map/pallas_call | solution.py:864
  77.9 1.0 %copy.10 = bf16[512,1024]{1,0:T(8,128)(2,1)} copy(bf16[512,1024]{1,0:T(8,128)(2,1)S(1)} %shard_map.82) | data formatting | bytes 2097152

commit v9 on v8

--- a/solution.py
+++ b/solution.py
@@ -323,6 +323,17 @@
             j_peer,
         )
 
+    def j_pair(r):
+        cols = pl.ds(pl.multiple_of(r * head_size, head_size), 2 * head_size)
+        return remote(
+            joined.at[0, :, cols], joined.at[1, :, cols], j_send.at[r], j_recv.at[r], j_peer
+        )
+
+    def all_j(wait):
+        wait(j_copy(0))
+        each((columns - 2) // 2, lambda i: wait(j_pair(2 * i + 1)))
+        wait(j_copy(columns - 1))
+
     def j_block(i):
         return remote(
             joined.at[0, block_rows(i)],
@@ -385,9 +396,9 @@
     def _(r):
         head(r)
 
-        @pl.when(middle)
-        def _():
-            j_copy(r).start()
+        @pl.when(middle & (r > 0) & (r % 2 == 0))
+        def _():
+            j_pair(r - 1).start()
 
     wide = groups * head_size
     joined[0, :, wide : wide + head_size] = (dk_acc[...] * scale).astype(jnp.bfloat16)
@@ -612,7 +623,7 @@
 
     @pl.when(middle)
     def _():
-        j_copy(groups).start()
+        j_pair(groups - 1).start()
         j_copy(groups + 1).start()
         each(pieces, lambda p: far_copy(p, piece_rows).start())
         steps = 3 * chunks
@@ -723,7 +734,7 @@
             def _():
                 core_sum(0, which(i - lag), (i - lag) % chunks, False)
 
-        each(columns, lambda r: j_copy(r).wait_recv())
+        all_j(lambda copy: copy.wait_recv())
 
         @pl.loop(0, chunks + 2)
         def _(k):
@@ -843,7 +854,7 @@
 
     @pl.when(middle)
     def _():
-        each(columns, lambda r: j_copy(r).wait_send())
+        all_j(lambda copy: copy.wait_send())
 
     @pl.when(ends)
     def _():

time: 79.1 us -> 79 us (level)
  no operation moved by 1% of the time
where the time goes in v9:
time: 79 us; the launch traced here: 78.8 us
  Pallas kernels  77.8 us (98%)
  local copies, waits for them, and re-layouts  0.97 us (1%)
    pallas_call x1, Pallas kernels, fused(): pl.pallas_call(functools.partial(fused_kernel, sides), out_shape=jax.Shap...  77.8 us

profile of v9, /device:TPU:17, one launch (start us, length us, event | category | flops | bytes accessed | tf_op | source)
XLA Modules:
  0.0 78.8 jit_solution(12960552355998341667)
XLA Ops:
  0.0 77.8 %shard_map.82 = bf16[512,1024]{1,0:T(8,128)(2,1)S(1)} custom-call(bf16[512,1024]{1,0:T(8,128)(2,1)} %bitcast.9, bf16[512,128]{1,0:T(8,128)(2,1)} %bitcast.11, bf16[512,128]{1,0:T(8,128)(2,1)} %bitcast.12, bf16[512,1024]{1,0:T(8,128)(2,1)} %bitcast.10, bf16[8,512]{1,0:T(8,128)(2,1)} %bitcast.14, bf16[8,512]{1,0:T(8,128)(2,1)} %bitcast.15, ...), custom_call_target="tpu_custom_call" | custom-call | tf_op jit(solution)/shard_map/pallas_call | solution.py:875
  77.8 1.0 %copy.10 = bf16[512,1024]{1,0:T(8,128)(2,1)} copy(bf16[512,1024]{1,0:T(8,128)(2,1)S(1)} %shard_map.82) | data formatting | bytes 2097152

commit v10 on v9

--- a/solution.py
+++ b/solution.py
@@ -230,7 +230,7 @@
     ]
     barrier = pltpu.get_barrier_semaphore()
     cross_peer = device(partner, y, xo, co)
-    peers = (y_peer, far_peer, j_peer, core_peer, x_peer, back_peer, cross_peer)
+    peers = (far_peer, cross_peer, j_peer, back_peer, y_peer, x_peer, core_peer)
     for peer in peers:
         pl.semaphore_signal(barrier, inc=1, device_id=peer, device_id_type=MESH)
 

time: 79 us -> 79 us (level)
  no operation moved by 1% of the time
where the time goes in v10:
time: 79 us; the launch traced here: 78.8 us
  Pallas kernels  77.8 us (98%)
  local copies, waits for them, and re-layouts  0.97 us (1%)
    pallas_call x1, Pallas kernels, fused(): pl.pallas_call(functools.partial(fused_kernel, sides), out_shape=jax.Shap...  77.8 us

profile of v10, /device:TPU:17, one launch (start us, length us, event | category | flops | bytes accessed | tf_op | source)
XLA Modules:
  0.0 78.8 jit_solution(15428670366769609816)
XLA Ops:
  0.0 77.8 %shard_map.82 = bf16[512,1024]{1,0:T(8,128)(2,1)S(1)} custom-call(bf16[512,1024]{1,0:T(8,128)(2,1)} %bitcast.9, bf16[512,128]{1,0:T(8,128)(2,1)} %bitcast.11, bf16[512,128]{1,0:T(8,128)(2,1)} %bitcast.12, bf16[512,1024]{1,0:T(8,128)(2,1)} %bitcast.10, bf16[8,512]{1,0:T(8,128)(2,1)} %bitcast.14, bf16[8,512]{1,0:T(8,128)(2,1)} %bitcast.15, ...), custom_call_target="tpu_custom_call" | custom-call | tf_op jit(solution)/shard_map/pallas_call | solution.py:875
  77.8 1.0 %copy.10 = bf16[512,1024]{1,0:T(8,128)(2,1)} copy(bf16[512,1024]{1,0:T(8,128)(2,1)S(1)} %shard_map.82) | data formatting | bytes 2097152
